TPU v7x, 128 devices: a whole 4x4x4 slice. The times are simulated.
128 devices in a mesh: dp: 1, sp: 128 (over z, y, x, core).
Axes of the slice: x: 4, y: 4, z: 4, core: 2. Of those that a mesh axis runs over, the one named last changes fastest.
Arguments:
- x_one: bfloat16 [2048, 7168], P(('dp', 'sp'))
- seg_one: int32 [2048], P(('dp', 'sp'))
- pos_one: int32 [2048], P(('dp', 'sp'))
- x_two: bfloat16 [2048, 7168], P(('dp', 'sp'))
- seg_two: int32 [2048], P(('dp', 'sp'))
- pos_two: int32 [2048], P(('dp', 'sp'))
- w_qdown: bfloat16 [7168, 1536], replicated
- gain_q: bfloat16 [1536], replicated
- w_qup: bfloat16 [1536, 24576], replicated
- w_kvdown: bfloat16 [7168, 576], replicated
- gain_kv: bfloat16 [512], replicated
- w_kvup: bfloat16 [512, 32768], replicated
- w_out: bfloat16 [16384, 7168], replicated
Outputs:
- output 1: bfloat16 [2048, 7168], P(('dp', 'sp'))
- output 2: bfloat16 [2048, 7168], P(('dp', 'sp'))
All inputs are finite; a program needn't handle non-finite values.
Results may differ from a plain program's by a relative error of at most 0.0140363.
Values are sent between devices in bfloat16 or wider.
A program may use at most 1.5 GiB of HBM per device.

v0:
```python
import jax
import jax.numpy as jnp
from jax import lax
from jax.sharding import PartitionSpec as P

NOPE_DIM = 128
ROPE_DIM = 64
KV_LAT = 512
V_DIM = 128
QK_DIM = NOPE_DIM + ROPE_DIM
ROPE_BASE = 10000.0
NORM_EPS = 1e-6


def rms_scale(pre_norm, gain_vec):
    mean_sq = jnp.mean(pre_norm * pre_norm, axis=-1, keepdims=True)
    return (pre_norm * lax.rsqrt(mean_sq + NORM_EPS) * gain_vec.astype(jnp.float32)).astype(jnp.bfloat16)


def rope_tables(positions):
    half_dim = ROPE_DIM // 2
    inv_freq = ROPE_BASE ** (-jnp.arange(half_dim, dtype=jnp.float32) / half_dim)
    angles = positions.astype(jnp.float32)[..., None] * inv_freq
    return jnp.cos(angles), jnp.sin(angles)


def rope_rotate(rot_in, cos_tab, sin_tab):
    half_dim = ROPE_DIM // 2
    first_half = rot_in[..., :half_dim]
    second_half = rot_in[..., half_dim:]
    return jnp.concatenate([first_half * cos_tab - second_half * sin_tab, second_half * cos_tab + first_half * sin_tab], axis=-1)


def latent_stage(x_local, pos_local, w_qdown, gain_q, w_kvdown, gain_kv):
    q_latent = rms_scale(jnp.dot(x_local, w_qdown, preferred_element_type=jnp.float32), gain_q)
    kv_raw = jnp.dot(x_local, w_kvdown, preferred_element_type=jnp.float32)
    kv_latent = rms_scale(kv_raw[:, :KV_LAT], gain_kv)
    cos_tab, sin_tab = rope_tables(pos_local)
    k_rope = rope_rotate(kv_raw[:, KV_LAT:], cos_tab, sin_tab).astype(jnp.bfloat16)
    return q_latent, kv_latent, k_rope


def head_attention(q_latent, kv_latent, k_rope, prompt_ids, positions, w_qup_cols, w_kvup_cols):
    num_tok = q_latent.shape[0]
    q_full = jnp.dot(q_latent, w_qup_cols, preferred_element_type=jnp.float32).reshape(num_tok, -1, QK_DIM)
    cos_tab, sin_tab = rope_tables(positions)
    q_nope = q_full[..., :NOPE_DIM].astype(jnp.bfloat16)
    q_rope = rope_rotate(q_full[..., NOPE_DIM:], cos_tab[:, None], sin_tab[:, None]).astype(jnp.bfloat16)
    kv_full = jnp.dot(kv_latent, w_kvup_cols, preferred_element_type=jnp.float32).astype(jnp.bfloat16).reshape(num_tok, -1, NOPE_DIM + V_DIM)
    scores = jnp.einsum('qhd,khd->hqk', q_nope, kv_full[..., :NOPE_DIM], preferred_element_type=jnp.float32)
    scores = scores + jnp.einsum('qhr,kr->hqk', q_rope, k_rope, preferred_element_type=jnp.float32)
    allowed = (prompt_ids[:, None] == prompt_ids[None, :]) & (positions[None, :] <= positions[:, None])
    attn_prob = jax.nn.softmax(jnp.where(allowed[None], scores * QK_DIM ** -0.5, -1e30), axis=-1).astype(jnp.bfloat16)
    return jnp.einsum('hqk,khv->qhv', attn_prob, kv_full[..., NOPE_DIM:], preferred_element_type=jnp.float32).astype(jnp.bfloat16)


def solution(mesh):
    tok_spec = P(('dp', 'sp'), None)
    idx_spec = P(('dp', 'sp'))
    col_spec = P(None, 'sp')

    def micro_block(x_local, seg_local, pos_local, w_qdown, gain_q, w_qup_cols, w_kvdown, gain_kv, w_kvup_cols, w_out):
        q_latent, kv_latent, k_rope = latent_stage(x_local, pos_local, w_qdown, gain_q, w_kvdown, gain_kv)
        q_all = lax.all_gather(q_latent, 'sp', axis=0, tiled=True)
        kv_all = lax.all_gather(kv_latent, 'sp', axis=0, tiled=True)
        rope_all = lax.all_gather(k_rope, 'sp', axis=0, tiled=True)
        seg_all = lax.all_gather(seg_local, 'sp', axis=0, tiled=True)
        pos_all = lax.all_gather(pos_local, 'sp', axis=0, tiled=True)
        head_out = head_attention(q_all, kv_all, rope_all, seg_all, pos_all, w_qup_cols, w_kvup_cols)
        tok_out = lax.all_to_all(head_out, 'sp', 0, 1, tiled=True)
        attn_flat = tok_out.reshape(tok_out.shape[0], -1)
        return jnp.dot(attn_flat, w_out, preferred_element_type=jnp.float32).astype(jnp.bfloat16)

    def local_body(x_one, seg_one, pos_one, x_two, seg_two, pos_two, w_qdown, gain_q, w_qup_cols, w_kvdown, gain_kv, w_kvup_cols, w_out):
        y_one = micro_block(x_one, seg_one, pos_one, w_qdown, gain_q, w_qup_cols, w_kvdown, gain_kv, w_kvup_cols, w_out)
        y_two = micro_block(x_two, seg_two, pos_two, w_qdown, gain_q, w_qup_cols, w_kvdown, gain_kv, w_kvup_cols, w_out)
        return y_one, y_two

    return jax.shard_map(local_body, mesh=mesh, in_specs=(tok_spec, idx_spec, idx_spec, tok_spec, idx_spec, idx_spec, P(), P(), col_spec, P(), P(), col_spec, P()), out_specs=(tok_spec, tok_spec), check_vma=False)
```

profile of v0, /device:TPU:1, one launch (start us, length us, event | category | flops | bytes accessed | tf_op | source)
XLA Modules:
  0.0 543.2 jit_solution(13308214091173100225)
XLA Ops:
  7.2 0.0 copy-start
  7.2 0.0 all-gather.9.cloned.1.call-start
  7.2 5.8 %fusion.88 = f32[16,576]{1,0:T(8,128)S(1)} fusion(bf16[16,7168]{1,0:T(8,128)(2,1)} %param.13, bf16[7168,576]{0,1:T(8,128)(2,1)} %param.22), kind=kOutput, calls=%fused_computation.119 | convolution fusion | flops 132120576 | bytes 8523776 | tf_op jit(solution)/shard_map/dot_general | solution.py:36
  13.0 5.6 %fusion.89 = f32[16,576]{1,0:T(8,128)S(1)} fusion(bf16[16,7168]{1,0:T(8,128)(2,1)S(1)} %copy-done, bf16[7168,576]{0,1:T(8,128)(2,1)} %param.22), kind=kOutput, calls=%fused_computation.120 | convolution fusion | flops 132120576 | bytes 8523776 | tf_op jit(solution)/shard_map/dot_general | solution.py:36
  18.6 0.1 multiply_reduce_fusion.2
  18.7 0.1 multiply_reduce_fusion.3
  18.9 0.7 multiply_convert_fusion.2
  19.6 0.0 all-gather.9.cloned.1.call-update
  19.6 0.0 all-gather.5.cloned.1.call-start
  19.7 0.7 all-gather.5.cloned.1.call-update
  20.4 0.0 all-gather.11.cloned.1.call-start
  20.4 8.9 %multiply_reduce_fusion = (f32[16]{0:T(128)S(1)}, f32[16,1536]{1,0:T(8,128)S(1)}) fusion(bf16[16,7168]{1,0:T(8,128)(2,1)S(1)} %copy-done, bf16[7168,1536]{1,0:T(8,128)(2,1)} %param.19), kind=kOutput, calls=%fused_computation.77 | convolution fusion | flops 352370688 | bytes 22347840 | tf_op jit(solution)/shard_map/dot_general | solution.py:35
  29.4 0.0 copy-start.7
  29.4 0.0 copy-start.8
  29.4 0.0 copy-start.9
  29.4 0.0 copy-start.10
  29.4 8.9 %multiply_reduce_fusion.1 = (f32[16]{0:T(128)S(1)}, f32[16,1536]{1,0:T(8,128)S(1)}) fusion(bf16[16,7168]{1,0:T(8,128)(2,1)S(1)} %copy-done.3, bf16[7168,1536]{1,0:T(8,128)(2,1)} %param.19), kind=kOutput, calls=%fused_computation.79 | convolution fusion | flops 352370688 | bytes 22347840 | tf_op jit(solution)/shard_map/dot_general | solution.py:35
  38.3 0.7 multiply_convert_fusion
  39.1 0.0 all-gather.11.cloned.1.call-update
  39.1 0.0 all-gather.7.cloned.1.call-start
  39.1 0.5 all-gather.7.cloned.1.call-update
  39.7 0.3 dynamic-update-slice.1
  40.0 0.3 dynamic-update-slice.3
  40.3 0.3 dynamic-update-slice
  40.5 0.3 dynamic-update-slice.2
  40.8 69.7 %all-reduce.4 = (s32[2048]{0:T(1024)S(1)}, s32[2048]{0:T(1024)S(1)}, s32[2048]{0:T(1024)S(1)}, s32[2048]{0:T(1024)S(1)}) all-reduce(s32[2048]{0:T(1024)S(1)} %dynamic-update-slice.1, s32[2048]{0:T(1024)S(1)} %dynamic-update-slice, s32[2048]{0:T(1024)S(1)} %dynamic-update-slice.3, ...), channel_id=1, replica_groups=mesh['dp'=1,'sp'=128] {'sp'}, use_global_device_ids=true, to_apply=%add.1 | all-reduce | flops 8192 | bytes 65536
  110.5 0.1 fusion.73
  110.7 0.1 pad_maximum_fusion.1
  110.7 0.1 pad_maximum_fusion
  110.8 34.2 %all_gather.39 = bf16[2048,64]{1,0:T(8,128)(2,1)S(1)} all-gather(bf16[16,64]{1,0:T(8,128)(2,1)S(1)} %pad_maximum_fusion.1), channel_id=1, replica_groups=mesh['dp'=1,'sp'=128] {'sp'}, dimensions={0}, use_global_device_ids=true | all-gather | bytes 264192 | tf_op jit(solution)/shard_map/all_gather | solution.py:66
  145.0 34.3 %all_gather.34 = bf16[2048,64]{1,0:T(8,128)(2,1)S(1)} all-gather(bf16[16,64]{1,0:T(8,128)(2,1)S(1)} %pad_maximum_fusion), channel_id=1, replica_groups=mesh['dp'=1,'sp'=128] {'sp'}, dimensions={0}, use_global_device_ids=true | all-gather | bytes 264192 | tf_op jit(solution)/shard_map/all_gather | solution.py:66
  179.3 3.3 fusion.11
  182.6 2.3 fusion.10
  184.9 39.2 %all-gather.11.cloned.1.call-done = bf16[2048,1536]{1,0:T(8,128)(2,1)} async-done(((bf16[16,1536]{1,0:T(8,128)(2,1)}), bf16[2048,1536]{1,0:T(8,128)(2,1)}) %all-gather.11.cloned.1.call-update) | async-done | bytes 6291472 | tf_op jit(solution)/shard_map/all_gather | solution.py:64
  224.1 6.5 %convolution_bitcast_fusion = f32[2048,1,192]{0,2,1:T(8,128)} fusion(bf16[2048,1536]{1,0:T(8,128)(2,1)} %all-gather.11.cloned.1.call-done, bf16[1536,24576]{1,0:T(8,128)(2,1)} %param.21, s32[]{:T(128)S(6)} %multiply.32), kind=kOutput, calls=%fused_computation.18 | convolution fusion | flops 1207959552 | bytes 8650756 | tf_op jit(solution)/shard_map/dot_general | solution.py:45
  230.6 62.7 %all-gather.7.cloned.1.call-done = bf16[2048,1536]{1,0:T(8,128)(2,1)} async-done(((bf16[16,1536]{1,0:T(8,128)(2,1)}), bf16[2048,1536]{1,0:T(8,128)(2,1)}) %all-gather.7.cloned.1.call-update) | async-done | bytes 6291472 | tf_op jit(solution)/shard_map/all_gather | solution.py:64
  293.4 5.4 convolution_bitcast_fusion.1
  298.7 3.8 fusion.63
  302.5 2.3 fusion.54
  304.9 9.7 %fusion.87 = (f32[2048]{0:T(1024)S(1)}, f32[1,2048,2048]{1,2,0:T(8,128)}) fusion(f32[2048,2048]{1,0:T(8,128)S(1)} %fusion.54, f32[2048,1,192]{0,2,1:T(8,128)} %convolution_bitcast_fusion, bf16[2048,1,256]{2,0,1:T(8,128)(2,1)} %fusion.11, s32[2048]{0:T(1024)S(1)} %get-tuple-element.4, s32[2048]{0:T(1024)S(1)} %get-tuple-element.5), kind=kOutput, calls=%fused_computation.118 | convolution fusion | flops 1103099904 | bytes 34643968 | tf_op jit(solution)/shard_map/qhd,khd->hqk/dot_general | solution.py:50
  314.5 8.2 %fusion.5 = f32[2048]{0:T(1024)S(1)} fusion(f32[1,2048,2048]{1,2,0:T(8,128)} %get-tuple-element.29, f32[2048]{0:T(1024)S(1)} %get-tuple-element.28), kind=kLoop, calls=%fused_computation.11 | loop fusion | flops 8386560 | bytes 16793600 | tf_op jit(solution)/shard_map/reduce_sum | solution.py:53
  322.7 7.5 %fusion.18 = bf16[2048,1,128]{0,2,1:T(8,128)(2,1)S(1)} fusion(f32[2048]{0:T(1024)S(1)} %fusion.5, f32[1,2048,2048]{1,2,0:T(8,128)} %get-tuple-element.29, f32[2048]{0:T(1024)S(1)} %get-tuple-element.28, bf16[2048,1,256]{2,0,1:T(8,128)(2,1)S(1)} %copy-done.4), kind=kOutput, calls=%fused_computation.26 | convolution fusion | flops 1086586880 | bytes 17842176 | tf_op jit(solution)/shard_map/hqk,khv->qhv/dot_general | solution.py:54
  330.3 0.5 broadcast.372
  330.8 1.0 reduce.5
  331.8 0.3 copy.36
  332.0 0.9 reshape.512
  333.0 5.6 %all-to-all-start.1 = ((bf16[128,2,1024]{2,1,0:T(2,128)(2,1)}), bf16[128,2,1024]{2,1,0:T(2,128)(2,1)S(1)}, u32[]{:S(2)}, u32[]{:S(2)}) async-start(bf16[128,2,1024]{2,1,0:T(2,128)(2,1)} %reshape.512), calls=%async_computation.1 | async-start | bytes 1048576 | tf_op jit(solution)/shard_map/all_to_all | solution.py:70
  338.6 2.3 fusion.50
  340.9 9.3 %fusion.86 = (f32[2048]{0:T(1024)S(1)}, f32[1,2048,2048]{1,2,0:T(8,128)}) fusion(f32[2048,2048]{1,0:T(8,128)S(1)} %fusion.50, f32[2048,1,192]{0,2,1:T(8,128)} %copy-done.2, bf16[2048,1,256]{2,0,1:T(8,128)(2,1)S(1)} %fusion.10, s32[2048]{0:T(1024)S(1)} %get-tuple-element.2, s32[2048]{0:T(1024)S(1)} %get-tuple-element.3), kind=kOutput, calls=%fused_computation.117 | convolution fusion | flops 1103099904 | bytes 34643968 | tf_op jit(solution)/shard_map/qhd,khd->hqk/dot_general | solution.py:50
  350.2 8.1 %fusion.4 = f32[2048]{0:T(1024)S(1)} fusion(f32[1,2048,2048]{1,2,0:T(8,128)} %get-tuple-element.27, f32[2048]{0:T(1024)S(1)} %get-tuple-element.26), kind=kLoop, calls=%fused_computation.10 | loop fusion | flops 8386560 | bytes 16793600 | tf_op jit(solution)/shard_map/reduce_sum | solution.py:53
  358.3 7.6 %fusion.21 = bf16[2048,1,128]{0,2,1:T(8,128)(2,1)S(1)} fusion(f32[2048]{0:T(1024)S(1)} %fusion.4, f32[1,2048,2048]{1,2,0:T(8,128)} %get-tuple-element.27, f32[2048]{0:T(1024)S(1)} %get-tuple-element.26, bf16[2048,1,256]{2,0,1:T(8,128)(2,1)S(1)} %fusion.10), kind=kOutput, calls=%fused_computation.27 | convolution fusion | flops 1086586880 | bytes 17842176 | tf_op jit(solution)/shard_map/hqk,khv->qhv/dot_general | solution.py:54
  365.9 1.0 reduce.4
  366.9 0.3 copy.35
  367.2 0.9 reshape.510
  368.1 10.1 %all-to-all-start = ((bf16[128,2,1024]{2,1,0:T(2,128)(2,1)}), bf16[128,2,1024]{2,1,0:T(2,128)(2,1)S(1)}, u32[]{:S(2)}, u32[]{:S(2)}) async-start(bf16[128,2,1024]{2,1,0:T(2,128)(2,1)} %reshape.510), calls=%async_computation | async-start | bytes 1048576 | tf_op jit(solution)/shard_map/all_to_all | solution.py:70
  378.2 0.5 reshape.513
  378.7 0.1 copy.24
  378.7 0.1 copy.22
  378.9 12.6 %all-to-all-done = bf16[128,2,1024]{2,1,0:T(2,128)(2,1)S(1)} async-done(((bf16[128,2,1024]{2,1,0:T(2,128)(2,1)}), bf16[128,2,1024]{2,1,0:T(2,128)(2,1)S(1)}, u32[]{:S(2)}, u32[]{:S(2)}) %all-to-all-start) | async-done | bytes 524320 | tf_op jit(solution)/shard_map/all_to_all | solution.py:70
  391.5 0.4 reshape.511
  392.0 0.1 copy.23
  392.0 0.1 copy.20
  392.2 72.0 %convolution_convert_fusion = bf16[16,7168]{1,0:T(8,128)(2,1)} fusion(bf16[16384,7168]{1,0:T(8,128)(2,1)} %param.25, bf16[2,8,128,128]{3,2,1,0:T(8,128)(2,1)S(1)} %bitcast.118), kind=kOutput, calls=%fused_computation.16 | convolution fusion | flops 3758211072 | bytes 235634688 | tf_op jit(solution)/shard_map/dot_general | solution.py:72
  464.2 72.0 %convolution_convert_fusion.1 = bf16[16,7168]{1,0:T(8,128)(2,1)} fusion(bf16[16384,7168]{1,0:T(8,128)(2,1)} %param.25, bf16[2,8,128,128]{3,2,1,0:T(8,128)(2,1)S(1)} %bitcast.119), kind=kOutput, calls=%fused_computation.17 | convolution fusion | flops 3758211072 | bytes 235634688 | tf_op jit(solution)/shard_map/dot_general | solution.py:72
  (33 shorter events, 0.1 us)
Async XLA Ops:
  7.2 5.9 %copy-start = (bf16[16,7168]{1,0:T(8,128)(2,1)S(1)}, bf16[16,7168]{1,0:T(8,128)(2,1)}, u32[]{:S(2)}) copy-start(bf16[16,7168]{1,0:T(8,128)(2,1)} %param.16) | copy-start | bytes 688132
  7.2 11.7 %copy-start.6 = (bf16[512]{0:T(512)(128)(2,1)S(1)}, bf16[512]{0:T(512)(128)(2,1)}, u32[]{:S(2)}) copy-start(bf16[512]{0:T(512)(128)(2,1)} %param.23) | copy-start | bytes 3076
  7.2 13.2 %copy-start.5 = (bf16[1536]{0:T(1024)(128)(2,1)S(1)}, bf16[1536]{0:T(1024)(128)(2,1)}, u32[]{:S(2)}) copy-start(bf16[1536]{0:T(1024)(128)(2,1)} %param.20) | copy-start | bytes 9220
  7.2 172.1 %all-gather.9.cloned.1.call-start = ((), (), s32[]{:S(2)}) async-start(), calls=%async_computation.4 | async-start | bytes 2113536 | tf_op jit(solution)/shard_map/all_gather | solution.py:65
  18.6 10.7 %copy-start.3 = (bf16[16,7168]{1,0:T(8,128)(2,1)S(1)}, bf16[16,7168]{1,0:T(8,128)(2,1)}, u32[]{:S(2)}) copy-start(bf16[16,7168]{1,0:T(8,128)(2,1)} %param.13) | copy-start | bytes 688132
  19.6 163.0 %all-gather.5.cloned.1.call-start = ((), (), s32[]{:S(2)}) async-start(), calls=%async_computation.2 | async-start | bytes 2113536 | tf_op jit(solution)/shard_map/all_gather | solution.py:65
  20.4 203.7 %all-gather.11.cloned.1.call-start = ((), (), s32[]{:S(2)}) async-start(), calls=%async_computation.5 | async-start | bytes 6340608 | tf_op jit(solution)/shard_map/all_gather | solution.py:64
  29.4 10.3 %copy-start.7 = (s32[16]{0:T(128)S(1)}, s32[16]{0:T(128)}, u32[]{:S(2)}) copy-start(s32[16]{0:T(128)} %param.15) | copy-start | bytes 196
  29.4 10.3 %copy-start.8 = (s32[16]{0:T(128)S(1)}, s32[16]{0:T(128)}, u32[]{:S(2)}) copy-start(s32[16]{0:T(128)} %param.18) | copy-start | bytes 196
  29.4 10.9 %copy-start.9 = (s32[16]{0:T(128)S(1)}, s32[16]{0:T(128)}, u32[]{:S(2)}) copy-start(s32[16]{0:T(128)} %param.14) | copy-start | bytes 196
  29.4 11.2 %copy-start.10 = (s32[16]{0:T(128)S(1)}, s32[16]{0:T(128)}, u32[]{:S(2)}) copy-start(s32[16]{0:T(128)} %param.17) | copy-start | bytes 196
  39.1 254.3 %all-gather.7.cloned.1.call-start = ((), (), s32[]{:S(2)}) async-start(), calls=%async_computation.3 | async-start | bytes 6340608 | tf_op jit(solution)/shard_map/all_gather | solution.py:64
  298.7 6.1 %copy-start.2 = (f32[2048,1,192]{0,2,1:T(8,128)}, f32[2048,1,192]{0,2,1:T(8,128)S(1)}, u32[]{:S(2)}) copy-start(f32[2048,1,192]{0,2,1:T(8,128)S(1)} %convolution_bitcast_fusion.1) | copy-start | bytes 4718596
  314.5 8.2 %copy-start.4 = (bf16[2048,1,256]{2,0,1:T(8,128)(2,1)S(1)}, bf16[2048,1,256]{2,0,1:T(8,128)(2,1)}, u32[]{:S(2)}) copy-start(bf16[2048,1,256]{2,0,1:T(8,128)(2,1)} %fusion.11) | copy-start | bytes 3145732
  333.0 35.1 %all-to-all-start.1 = ((bf16[128,2,1024]{2,1,0:T(2,128)(2,1)}), bf16[128,2,1024]{2,1,0:T(2,128)(2,1)S(1)}, u32[]{:S(2)}, u32[]{:S(2)}) async-start(bf16[128,2,1024]{2,1,0:T(2,128)(2,1)} %reshape.512), calls=%async_computation.1 | async-start | bytes 1048576 | tf_op jit(solution)/shard_map/all_to_all | solution.py:70
  368.1 23.4 %all-to-all-start = ((bf16[128,2,1024]{2,1,0:T(2,128)(2,1)}), bf16[128,2,1024]{2,1,0:T(2,128)(2,1)S(1)}, u32[]{:S(2)}, u32[]{:S(2)}) async-start(bf16[128,2,1024]{2,1,0:T(2,128)(2,1)} %reshape.510), calls=%async_computation | async-start | bytes 1048576 | tf_op jit(solution)/shard_map/all_to_all | solution.py:70
  464.2 72.0 %copy-start.1 = (bf16[16,7168]{1,0:T(8,128)(2,1)S(1)}, bf16[16,7168]{1,0:T(8,128)(2,1)}, u32[]{:S(2)}) copy-start(bf16[16,7168]{1,0:T(8,128)(2,1)} %param.16) | copy-start | bytes 688132
Sparse Core Ops, SparseCore 0:
  19.7 69.0 all-gather.8
  91.9 62.7 all-gather.4
  158.4 65.6 all-gather.10
  227.6 65.6 all-gather.6
where the time goes:
time: 551 us; the launch traced here: 543 us
  matrix products  229 us (42%)
  blocking collectives  138 us (25%)
  waiting for transfers between devices  116 us (21%)
  other arithmetic  24 us (4%)
  starting transfers between devices  15.9 us (3%)
  between operations  14.5 us (3%)
    dot_general x2, matrix products, micro_block(): jnp.dot(attn_flat, w_out, preferred_element_type=jnp.float32)  144 us
    all_gather x2, waiting for transfers between devices, micro_block(): q_all = lax.all_gather(q_latent, 'sp', axis=0, tiled=True)  102 us
    unnamed x1, blocking collectives  69.7 us
    all_gather x2, blocking collectives, micro_block(): rope_all = lax.all_gather(k_rope, 'sp', axis=0, tiled=True)  68.5 us
    dot_general x2, matrix products, head_attention(): jnp.einsum('qhd,khd->hqk', q_nope, kv_full[..., :NOPE_DIM], preferred_ele...  19 us
    dot_general x2, matrix products, latent_stage(): jnp.dot(x_local, w_qdown, preferred_element_type=jnp.float32)  17.8 us
    reduce_sum x2, other arithmetic, head_attention(): jax.nn.softmax(jnp.where(allowed[None], scores * QK_DIM ** (-0.5), -1e+30...  16.2 us
    all_to_all x2, starting transfers between devices, micro_block(): tok_out = lax.all_to_all(head_out, 'sp', 0, 1, tiled=True)  15.8 us
  transfers between devices with their start and end apart: 6, of which 3 were waited for; matrix products, arithmetic and copies ran while one was open for 11% of the time, Pallas kernels for 0%

commit v1 on v0

v1 whole, which is shorter than its diff:
```python
import functools

import jax
import jax.numpy as jnp
from jax import lax
from jax.experimental import pallas as pl
from jax.experimental.pallas import tpu as pltpu
from jax.sharding import PartitionSpec as P

D_MODEL = 7168
HEADS = 128
Q_LAT = 1536
KV_LAT = 512
ROPE_DIM = 64
NOPE_DIM = 128
V_DIM = 128
QK_DIM = NOPE_DIM + ROPE_DIM
ROPE_BASE = 10000.0
NORM_EPS = 1e-6

ROWS = 16
RING = 4
GROUP = 2 * RING
G_HEADS = HEADS // GROUP
TOKENS = 2048
KV_W = 2 * KV_LAT + 2 * ROPE_DIM
Q_W = KV_LAT + 2 * ROPE_DIM
MESH = pl.DeviceIdType.MESH

COLORS = (((0, 384), (2, 1, 0)), ((384, 768), (1, 0, 2)), ((768, 1152), (0, 2, 1)))


def coords():
    me = lax.axis_index("sp")
    return me // 32, lax.rem(me // 8, 4), lax.rem(me // 2, 4), lax.rem(me, 2)


def device(z, y, x, c):
    return {"sp": ((z * RING + y) * RING + x) * 2 + c}


def shifted(pos, axis, k):
    out = list(pos)
    out[axis] = lax.rem(pos[axis] + k, RING)
    return tuple(out)


def gather_kernel(kv_in, q_in, tab_in, kv_ref, q_ref, tab_ref, kv_send, kv_recv, q_send, q_recv, t_send, t_recv,
                  d_send, d_recv, dq_send, dq_recv):
    z, y, x, c = coords()
    pos = (z, y, x)
    other = device(z, y, x, 1 - c)

    barrier = pltpu.get_barrier_semaphore()
    for axis in range(3):
        for k in range(1, RING):
            pl.semaphore_signal(barrier, inc=1, device_id=device(*shifted(pos, axis, k), c), device_id_type=MESH)
    pl.semaphore_signal(barrier, inc=1, device_id=other, device_id_type=MESH)
    kv_ref[z, y, x, c] = kv_in[...]
    q_ref[:, z, c] = q_in[...]
    tab_ref[:, z, c] = tab_in[...]
    pl.semaphore_wait(barrier, 10)

    def kv_piece(color, phase, at):
        (lo, hi), order = COLORS[color]
        index = [at[0], at[1], at[2]]
        for axis in order[:phase]:
            index[axis] = slice(None)
        return kv_ref.at[index[0], index[1], index[2], c, :, pl.ds(lo, hi - lo)]

    def kv_copy(color, phase, k, at, to):
        piece = kv_piece(color, phase, at)
        return pltpu.make_async_remote_copy(
            src_ref=piece, dst_ref=piece, send_sem=kv_send.at[color, phase, k - 1],
            recv_sem=kv_recv.at[color, phase, k - 1], device_id=to, device_id_type=MESH)

    def pass_copy(color, k, at):
        piece = kv_piece(color, 2, at)
        return pltpu.make_async_remote_copy(
            src_ref=piece, dst_ref=piece, send_sem=d_send.at[color, k],
            recv_sem=d_recv.at[color, k], device_id=other, device_id_type=MESH)

    def other_piece(color, k, at):
        (lo, hi), order = COLORS[color]
        index = [slice(None)] * 3
        index[order[2]] = at[order[2]]
        piece = kv_ref.at[index[0], index[1], index[2], 1 - c, :, pl.ds(lo, hi - lo)]
        return pltpu.make_async_remote_copy(
            src_ref=piece, dst_ref=piece, send_sem=d_send.at[color, k],
            recv_sem=d_recv.at[color, k], device_id=other, device_id_type=MESH)

    def q_copy(k, zz, cc, to, send, recv):
        return pltpu.make_async_remote_copy(
            src_ref=q_ref.at[:, zz, cc], dst_ref=q_ref.at[:, zz, cc], send_sem=send, recv_sem=recv,
            device_id=to, device_id_type=MESH)

    def t_copy(k, zz, cc, to, send, recv):
        return pltpu.make_async_remote_copy(
            src_ref=tab_ref.at[:, zz, cc], dst_ref=tab_ref.at[:, zz, cc], send_sem=send, recv_sem=recv,
            device_id=to, device_id_type=MESH)

    for phase in range(3):
        for color in range(3):
            axis = COLORS[color][1][phase]
            for k in range(1, RING):
                kv_copy(color, phase, k, pos, device(*shifted(pos, axis, k), c)).start()
        if phase == 0:
            for k in range(1, RING):
                to = device(*shifted(pos, 0, k), c)
                t_copy(k, z, c, to, t_send.at[k - 1], t_recv.at[k - 1]).start()
                q_copy(k, z, c, to, q_send.at[k - 1], q_recv.at[k - 1]).start()
            t_copy(0, z, c, other, dq_send.at[0, 0], dq_recv.at[0, 0]).start()
            q_copy(0, z, c, other, dq_send.at[1, 0], dq_recv.at[1, 0]).start()
        if phase == 2:
            for color in range(3):
                pass_copy(color, 0, pos).start()
            for k in range(1, RING):
                zz = lax.rem(z + RING - k, RING)
                t_copy(k, zz, c, other, t_send.at[k - 1], t_recv.at[k - 1]).wait_recv()
                t_copy(k, zz, c, other, dq_send.at[0, k], dq_recv.at[0, k]).start()
                q_copy(k, zz, c, other, q_send.at[k - 1], q_recv.at[k - 1]).wait_recv()
                q_copy(k, zz, c, other, dq_send.at[1, k], dq_recv.at[1, k]).start()
        for k in (1, 3, 2):
            for color in range(3):
                axis = COLORS[color][1][phase]
                source = shifted(pos, axis, RING - k)
                kv_copy(color, phase, k, source, other).wait_recv()
                if phase == 2:
                    pass_copy(color, k, source).start()

    for k in range(RING):
        zz = lax.rem(z + RING - k, RING)
        t_copy(k, zz, 1 - c, other, dq_send.at[0, k], dq_recv.at[0, k]).wait()
        q_copy(k, zz, 1 - c, other, dq_send.at[1, k], dq_recv.at[1, k]).wait()
        for color in range(3):
            source = shifted(pos, COLORS[color][1][2], RING - k)
            other_piece(color, k, source).wait()
    for k in range(1, RING):
        t_copy(k, z, c, other, t_send.at[k - 1], t_recv.at[k - 1]).wait_send()
        q_copy(k, z, c, other, q_send.at[k - 1], q_recv.at[k - 1]).wait_send()
        for phase in range(3):
            for color in range(3):
                kv_copy(color, phase, k, pos, other).wait_send()


def gather(kv_loc, q_loc, tab_loc):
    dma = pltpu.SemaphoreType.DMA
    vmem = pl.BlockSpec(memory_space=pltpu.VMEM)
    return pl.pallas_call(
        gather_kernel,
        out_shape=(jax.ShapeDtypeStruct((RING, RING, RING, 2, ROWS, KV_W), jnp.bfloat16),
                   jax.ShapeDtypeStruct((2, RING, 2, ROWS, Q_LAT), jnp.bfloat16),
                   jax.ShapeDtypeStruct((2, RING, 2, ROWS, 128), jnp.float32)),
        in_specs=[vmem] * 3,
        out_specs=(vmem,) * 3,
        scratch_shapes=[dma((3, 3, 3)), dma((3, 3, 3)), dma((3,)), dma((3,)), dma((3,)), dma((3,)),
                        dma((3, 4)), dma((3, 4)), dma((2, 4)), dma((2, 4))],
        compiler_params=pltpu.CompilerParams(collective_id=0, has_side_effects=True),
        name="latent_gather",
    )(kv_loc, q_loc, tab_loc)


WQ_CHUNKS = 4


def attention_kernel(q_ref, tab_ref, kv_ref, wq_hbm, wkv_hbm, o_ref, wq, wkv, q_eff, o_lat, wq_sem, wkv_sem):
    z, y, x, c = coords()
    rank = z * 2 + c
    rows = 2 * RING * 2 * ROWS
    unit_rows = 2 * ROWS
    wcols = G_HEADS * QK_DIM // WQ_CHUNKS

    def wq_copy(i):
        return pltpu.make_async_copy(
            wq_hbm.at[:, pl.ds(pl.multiple_of(rank * (G_HEADS * QK_DIM) + i * wcols, 128), wcols)],
            wq.at[i], wq_sem.at[i])

    wkv_copy = pltpu.make_async_copy(
        wkv_hbm.at[:, pl.ds(pl.multiple_of(rank * (G_HEADS * 256), 128), G_HEADS * 256)], wkv, wkv_sem)
    wq_copy(0).start()
    wkv_copy.start()
    for i in range(1, WQ_CHUNKS):
        wq_copy(i).start()

    lane = lax.broadcasted_iota(jnp.int32, (rows, 128), 1)
    tab = tab_ref[...]
    cos_t = jnp.where(lane < 32, tab, jnp.where(lane < 64, pltpu.roll(tab, 32, 1), 0.0))
    sin_b = jnp.where((lane >= 32) & (lane < 64), tab, 0.0)
    sin_a = jnp.where(lane < 32, -pltpu.roll(tab, 96, 1), 0.0)

    def put_rope(head, part):
        out = part * cos_t + pltpu.roll(part, 32, 1) * sin_b + pltpu.roll(part, 96, 1) * sin_a
        half = rows // 2
        out = jnp.concatenate([out[:half], pltpu.roll(out[half:], 64, 1)], axis=0)
        q_eff[:, head, :, KV_LAT:] = out.astype(jnp.bfloat16).reshape(2 * RING, unit_rows, 128)

    def put_nope(head, part):
        w_k = wkv[:, pl.ds(pl.multiple_of(head * 256, 256), 128)]
        out = lax.dot_general(part.astype(jnp.bfloat16), w_k, (((1,), (1,)), ((), ())), preferred_element_type=jnp.float32)
        q_eff[:, head, :, :KV_LAT] = out.astype(jnp.bfloat16).reshape(2 * RING, unit_rows, KV_LAT)

    pairs = wcols // (2 * QK_DIM)
    for i in range(WQ_CHUNKS):
        wq_copy(i).wait()
        if i == 0:
            wkv_copy.wait()

        @pl.loop(0, pairs)
        def _(p):
            cols = pl.ds(pl.multiple_of(p * (2 * QK_DIM), 128), 2 * QK_DIM)
            f = jnp.dot(q_ref[...], wq[i, :, cols], preferred_element_type=jnp.float32)
            head = (i * pairs + p) * 2
            put_nope(head, f[:, :128])
            put_rope(head, f[:, 128:256])
            mid = pltpu.roll(f[:, 128:256], 64, 1)
            last = pltpu.roll(f[:, 256:384], 64, 1)
            put_nope(head + 1, jnp.where(lane < 64, mid, last))
            put_rope(head + 1, last)

    chunk_heads = 8
    scale2 = (QK_DIM ** -0.5) * 1.4426950408889634
    tok = lax.broadcasted_iota(jnp.int32, (unit_rows, 1), 0)
    for zz in range(RING):
        length = (zz + 1) * 512
        key = lax.broadcasted_iota(jnp.int32, (unit_rows, length), 1)
        q_tok = zz * 512 + y * 128 + x * 32 + tok

        for mb in range(2):
            unit = mb * RING + zz
            p0 = tab_ref[unit * unit_rows:(unit + 1) * unit_rows, 64:65].astype(jnp.int32)
            cap = jnp.where((key <= q_tok) & (key >= q_tok - p0), 3e38, -1e30).astype(jnp.float32)

            @pl.loop(0, G_HEADS // chunk_heads)
            def _(j):
                heads = pl.ds(j * chunk_heads, chunk_heads)
                q = q_eff[unit, heads].reshape(chunk_heads * unit_rows, Q_W)
                keys = kv_ref[:length, mb * KV_LAT:(mb + 1) * KV_LAT]
                trans = (((1,), (1,)), ((), ()))
                s = lax.dot_general(q[:, :KV_LAT], keys, trans, preferred_element_type=jnp.float32)
                s = s + lax.dot_general(q[:, KV_LAT:], kv_ref[:length, 2 * KV_LAT:], trans, preferred_element_type=jnp.float32)
                s = jnp.minimum(s.reshape(chunk_heads, unit_rows, length), cap[None])
                top = jnp.max(s, axis=-1, keepdims=True)
                e = jnp.exp2((s - top) * scale2)
                total = jnp.sum(e, axis=-1, keepdims=True)
                e = e.astype(jnp.bfloat16).reshape(chunk_heads * unit_rows, length)
                o = jnp.dot(e, keys, preferred_element_type=jnp.float32).reshape(chunk_heads, unit_rows, KV_LAT)
                o_lat[heads, unit * unit_rows:(unit + 1) * unit_rows, :] = (o / total).astype(jnp.bfloat16)

    @pl.loop(0, G_HEADS)
    def _(h):
        w_v = wkv[:, pl.ds(pl.multiple_of(h * 256 + 128, 128), 128)]
        o_ref[:, pl.ds(pl.multiple_of(h * 128, 128), 128)] = jnp.dot(
            o_lat[h], w_v, preferred_element_type=jnp.float32).astype(jnp.bfloat16)


def attention(q_all, tab_all, kv_all, w_qup, w_kvup):
    rows = 2 * RING * 2 * ROWS
    vmem = pl.BlockSpec(memory_space=pltpu.VMEM)
    hbm = pl.BlockSpec(memory_space=pl.ANY)
    return pl.pallas_call(
        attention_kernel,
        out_shape=jax.ShapeDtypeStruct((rows, G_HEADS * V_DIM), jnp.bfloat16),
        in_specs=[vmem, vmem, vmem, hbm, hbm],
        out_specs=vmem,
        scratch_shapes=[
            pltpu.VMEM((WQ_CHUNKS, Q_LAT, G_HEADS * QK_DIM // WQ_CHUNKS), jnp.bfloat16),
            pltpu.VMEM((KV_LAT, G_HEADS * 256), jnp.bfloat16),
            pltpu.VMEM((2 * RING, G_HEADS, 2 * ROWS, Q_W), jnp.bfloat16),
            pltpu.VMEM((G_HEADS, rows, KV_LAT), jnp.bfloat16),
            pltpu.SemaphoreType.DMA((WQ_CHUNKS,)),
            pltpu.SemaphoreType.DMA,
        ],
        compiler_params=pltpu.CompilerParams(vmem_limit_bytes=60 * 2 ** 20),
        name="latent_attention",
    )(q_all, tab_all, kv_all, w_qup, w_kvup)


W_ROWS = 1024
W_SLOTS = 5
HALF_N = D_MODEL // 2
OUT_ROWS = 4 * ROWS


def out_kernel(o_ref, w_hbm, y_one, y_two, o_all, w_buf, acc, y_send, w_sem, a_send, a_recv, d_send, d_recv, y_ssem, y_rsem):
    z, y, x, c = coords()
    pos = (z, y, x)
    other = device(z, y, x, 1 - c)
    k_cols = G_HEADS * V_DIM
    per_rank = k_cols // W_ROWS
    steps = GROUP * per_rank

    order = ((0, 0), (0, 1), (1, 0), (3, 0), (1, 1), (2, 0), (3, 1), (2, 1))

    def rank_at(j):
        rank = jnp.int32(0)
        for i, (k, flip) in enumerate(order):
            cc = c if flip == 0 else 1 - c
            rank = jnp.where(j == i, lax.rem(z + RING - k, RING) * 2 + cc, rank)
        return rank

    def w_copy(t):
        rank = rank_at(t // per_rank)
        row = pl.multiple_of(rank * k_cols + lax.rem(t, per_rank) * W_ROWS, W_ROWS)
        slot = lax.rem(t, W_SLOTS)
        return pltpu.make_async_copy(
            w_hbm.at[pl.ds(row, W_ROWS), pl.ds(pl.multiple_of(c * HALF_N, 128), HALF_N)], w_buf.at[slot], w_sem.at[slot])

    barrier = pltpu.get_barrier_semaphore()
    for k in range(1, RING):
        pl.semaphore_signal(barrier, inc=1, device_id=device(*shifted(pos, 0, k), c), device_id_type=MESH)
    pl.semaphore_signal(barrier, inc=1, device_id=other, device_id_type=MESH)
    for t in range(W_SLOTS - 1):
        w_copy(jnp.int32(t)).start()
    pl.semaphore_wait(barrier, 4)

    me = z * 2 + c

    def ring_copy(k, src_rank, src_z, to):
        return pltpu.make_async_remote_copy(
            src_ref=o_ref.at[:, src_z], dst_ref=o_all.at[src_rank], send_sem=a_send.at[k - 1],
            recv_sem=a_recv.at[k - 1], device_id=to, device_id_type=MESH)

    def pass_copy(k, rank, src):
        return pltpu.make_async_remote_copy(
            src_ref=src, dst_ref=o_all.at[rank], send_sem=d_send.at[k], recv_sem=d_recv.at[k],
            device_id=other, device_id_type=MESH)

    for k in (1, 3, 2):
        zz = lax.rem(z + k, RING)
        ring_copy(k, me, zz, device(zz, y, x, c)).start()
    pass_copy(0, me, o_ref.at[:, z]).start()
    o_all[me] = o_ref[:, z]
    acc[...] = jnp.zeros_like(acc)

    @pl.loop(0, steps)
    def _(t):
        @pl.when(t + W_SLOTS - 1 < steps)
        def _():
            w_copy(t + W_SLOTS - 1).start()

        for i, (k, flip) in enumerate(order):
            if i == 0:
                continue

            @pl.when(t == i * per_rank)
            def _(i=i, k=k, flip=flip):
                zz = lax.rem(z + RING - k, RING)
                if flip == 0:
                    ring_copy(k, zz * 2 + c, z, other).wait_recv()
                    pass_copy(k, zz * 2 + c, o_all.at[zz * 2 + c]).start()
                else:
                    pass_copy(k, zz * 2 + 1 - c, o_all.at[zz * 2 + 1 - c]).wait_recv()

        rank = rank_at(t // per_rank)
        w_copy(t).wait()
        lhs = o_all[rank, :, :, :, pl.ds(pl.multiple_of(lax.rem(t, per_rank) * W_ROWS, W_ROWS), W_ROWS)].reshape(OUT_ROWS, W_ROWS)
        slot = lax.rem(t, W_SLOTS)
        step_n = 512
        for n in range(HALF_N // step_n):
            cols = slice(n * step_n, (n + 1) * step_n)
            acc[:, cols] += jnp.dot(lhs, w_buf[slot, :, cols], preferred_element_type=jnp.float32)

    acc4 = acc.reshape(2, 2, ROWS, HALF_N)
    my_cols = pl.ds(pl.multiple_of(c * HALF_N, 128), HALF_N)
    for mb, y_ref in enumerate((y_one, y_two)):
        y_send[mb] = acc4[mb, 1 - c].astype(jnp.bfloat16)
    for mb, y_ref in enumerate((y_one, y_two)):
        y_ref[:, my_cols] = acc4[mb, c].astype(jnp.bfloat16)

    def y_copy(mb, y_ref, cols):
        return pltpu.make_async_remote_copy(
            src_ref=y_send.at[mb], dst_ref=y_ref.at[:, cols], send_sem=y_ssem.at[mb], recv_sem=y_rsem.at[mb],
            device_id=other, device_id_type=MESH)

    for mb, y_ref in enumerate((y_one, y_two)):
        y_copy(mb, y_ref, my_cols).start()
    their_cols = pl.ds(pl.multiple_of((1 - c) * HALF_N, 128), HALF_N)
    for mb, y_ref in enumerate((y_one, y_two)):
        y_copy(mb, y_ref, their_cols).wait()
    for k in range(1, RING):
        ring_copy(k, me, z, other).wait_send()
    for k in range(RING):
        pass_copy(k, me, o_all.at[me]).wait_send()


def project_out(o, w_out):
    dma = pltpu.SemaphoreType.DMA
    vmem = pl.BlockSpec(memory_space=pltpu.VMEM)
    hbm = pl.BlockSpec(memory_space=pl.ANY)
    y_shape = jax.ShapeDtypeStruct((ROWS, D_MODEL), jnp.bfloat16)
    return pl.pallas_call(
        out_kernel,
        out_shape=(y_shape, y_shape),
        in_specs=[vmem, hbm],
        out_specs=(vmem, vmem),
        scratch_shapes=[
            pltpu.VMEM((GROUP, 2, 2, ROWS, G_HEADS * V_DIM), jnp.bfloat16),
            pltpu.VMEM((W_SLOTS, W_ROWS, HALF_N), jnp.bfloat16),
            pltpu.VMEM((OUT_ROWS, HALF_N), jnp.float32),
            pltpu.VMEM((2, ROWS, HALF_N), jnp.bfloat16),
            dma((W_SLOTS,)), dma((3,)), dma((3,)), dma((4,)), dma((4,)), dma((2,)), dma((2,)),
        ],
        compiler_params=pltpu.CompilerParams(collective_id=1, has_side_effects=True, vmem_limit_bytes=60 * 2 ** 20),
        name="out_projection",
    )(o, w_out)


def rms_scale(pre_norm, gain_vec):
    mean_sq = jnp.mean(pre_norm * pre_norm, axis=-1, keepdims=True)
    return (pre_norm * lax.rsqrt(mean_sq + NORM_EPS) * gain_vec.astype(jnp.float32)).astype(jnp.bfloat16)


def latents(x_one, pos_one, x_two, pos_two, w_qdown, gain_q, w_kvdown, gain_kv):
    half_dim = ROPE_DIM // 2
    rows_x = jnp.concatenate([x_one, x_two], axis=0)
    pos = jnp.concatenate([pos_one, pos_two], axis=0).astype(jnp.float32)[:, None]
    q_latent = rms_scale(jnp.dot(rows_x, w_qdown, preferred_element_type=jnp.float32), gain_q)
    kv_raw = jnp.dot(rows_x, w_kvdown, preferred_element_type=jnp.float32)
    kv_latent = rms_scale(kv_raw[:, :KV_LAT], gain_kv)
    inv_freq = ROPE_BASE ** (-jnp.arange(half_dim, dtype=jnp.float32) / half_dim)
    angles = pos * inv_freq
    cos_tab, sin_tab = jnp.cos(angles), jnp.sin(angles)
    a, b = kv_raw[:, KV_LAT:KV_LAT + half_dim], kv_raw[:, KV_LAT + half_dim:]
    k_rope = jnp.concatenate([a * cos_tab - b * sin_tab, b * cos_tab + a * sin_tab], axis=-1).astype(jnp.bfloat16)
    kv_loc = jnp.concatenate([kv_latent[:ROWS], kv_latent[ROWS:], k_rope[:ROWS], k_rope[ROWS:]], axis=1)
    tab = jnp.concatenate([cos_tab, sin_tab, jnp.broadcast_to(pos, (2 * ROWS, ROPE_DIM))], axis=1)
    return kv_loc, q_latent.reshape(2, ROWS, Q_LAT), tab.reshape(2, ROWS, 128)


def solution(mesh):
    tok_spec = P(('dp', 'sp'), None)
    idx_spec = P(('dp', 'sp'))

    def local_body(x_one, seg_one, pos_one, x_two, seg_two, pos_two, w_qdown, gain_q, w_qup, w_kvdown, gain_kv, w_kvup, w_out):
        kv_loc, q_loc, tab_loc = latents(x_one, pos_one, x_two, pos_two, w_qdown, gain_q, w_kvdown, gain_kv)
        kv_all, q_all, tab_all = gather(kv_loc, q_loc, tab_loc)
        o = attention(q_all.reshape(-1, Q_LAT), tab_all.reshape(-1, 128), kv_all.reshape(TOKENS, KV_W), w_qup, w_kvup)
        return project_out(o.reshape(2, RING, 2, ROWS, -1), w_out)

    return jax.shard_map(local_body, mesh=mesh, in_specs=(tok_spec, idx_spec, idx_spec, tok_spec, idx_spec, idx_spec, P(), P(), P(), P(), P(), P(), P()), out_specs=(tok_spec, tok_spec), check_vma=False)
```

time: 551 us -> 141 us (0.26); the launches traced: 543 us -> 140 us
  matrix products: 229 us -> 15.1 us
  blocking collectives: 138 us -> 0 us
  waiting for transfers between devices: 116 us -> 0 us
  Pallas kernels: 0 us -> 113 us
  other arithmetic: 24 us -> 4.88 us
  starting transfers between devices: 15.9 us -> 0 us
  between operations: 14.5 us -> 0.69 us
    dot_general x16 -> x2, matrix products: 229 us -> 15.1 us  [the longest x1 9.34 us: latents(): jnp.dot(rows_x, w_qdown, preferred_element_type=jnp.float32)]
    pallas_call x0 -> x3, Pallas kernels: none -> 113 us  [the longest x1 40.1 us: attention(): pl.pallas_call(attention_kernel, out_shape=jax.ShapeDtypeStruct((rows, G_...]
    all_gather x4 -> x0, waiting for transfers between devices: 102 us -> none  [the longest x2 102 us: micro_block(): q_all = lax.all_gather(q_latent, 'sp', axis=0, tiled=True)]
    unnamed x1 -> x0, blocking collectives: 69.7 us -> none
    all_gather x2 -> x0, blocking collectives: 68.5 us -> none  [micro_block(): rope_all = lax.all_gather(k_rope, 'sp', axis=0, tiled=True)]
    reduce_sum x2 -> x0, other arithmetic: 16.2 us -> none  [head_attention(): jax.nn.softmax(jnp.where(allowed[None], scores * QK_DIM ** (-0.5), -1e+30...]
    all_to_all x2 -> x0, starting transfers between devices: 15.8 us -> none  [micro_block(): tok_out = lax.all_to_all(head_out, 'sp', 0, 1, tiled=True)]
    all_to_all x2 -> x0, waiting for transfers between devices: 12.6 us -> none  [micro_block(): tok_out = lax.all_to_all(head_out, 'sp', 0, 1, tiled=True)]
  transfers between devices with their start and end apart: 6 -> 0, of which waited for: 3 -> 0; matrix products, arithmetic and copies ran while one was open for 11% -> 0% of each run, Pallas kernels for 0% -> 0%
where the time goes in v1:
time: 141 us; the launch traced here: 140 us
  Pallas kernels  113 us (80%)
  matrix products  15.1 us (11%)
  local copies, waits for them, and re-layouts  6.05 us (4%)
  other arithmetic  4.88 us (3%)
    pallas_call x1, Pallas kernels, attention(): pl.pallas_call(attention_kernel, out_shape=jax.ShapeDtypeStruct((rows, G_...  40.1 us
    pallas_call x1, Pallas kernels, project_out(): pl.pallas_call(out_kernel, out_shape=(y_shape, y_shape), in_specs=[vmem,...  39.8 us
    pallas_call x1, Pallas kernels, gather(): pl.pallas_call(gather_kernel, out_shape=(jax.ShapeDtypeStruct((RING, RING...  33.5 us
    dot_general x1, matrix products, latents(): jnp.dot(rows_x, w_qdown, preferred_element_type=jnp.float32)  9.34 us
    dot_general x1, matrix products, latents(): kv_raw = jnp.dot(rows_x, w_kvdown, preferred_element_type=jnp.float32)  5.8 us
    unnamed x3, local copies, waits for them, and re-layouts  4.23 us

profile of v1, /device:TPU:1, one launch (start us, length us, event | category | flops | bytes accessed | tf_op | source)
XLA Modules:
  0.0 140.1 jit_solution(12636524690631680646)
XLA Ops:
  0.6 0.8 fusion.9
  1.4 0.1 convert_element_type.32
  1.5 0.7 add_convert_fusion
  2.2 0.7 convert_element_type.26
  2.9 0.7 convert_element_type.29
  3.6 0.1 broadcast_in_dim.2
  3.7 0.1 multiply_cosine_fusion
  3.8 0.7 pad_maximum_fusion.tab_in
  4.5 1.0 constant_dynamic-update-slice_fusion.1
  5.5 1.0 constant_dynamic-update-slice_fusion
  6.4 5.8 %fusion.11 = f32[32,576]{1,0:T(8,128)S(1)} fusion(bf16[32,7168]{1,0:T(8,128)(2,1)S(1)} %constant_dynamic-update-slice_fusion, bf16[7168,576]{0,1:T(8,128)(2,1)} %param.20), kind=kOutput, calls=%fused_computation.30 | convolution fusion | flops 264241152 | bytes 8790016 | tf_op jit(solution)/shard_map/dot_general | solution.py:418
  12.2 9.3 %multiply_reduce_fusion = (f32[32]{0:T(128)S(1)}, f32[32,1536]{1,0:T(8,128)S(1)}) fusion(bf16[32,7168]{1,0:T(8,128)(2,1)S(1)} %constant_dynamic-update-slice_fusion, bf16[7168,1536]{1,0:T(8,128)(2,1)} %param.17), kind=kOutput, calls=%fused_computation.1 | convolution fusion | flops 704741376 | bytes 22675584 | tf_op jit(solution)/shard_map/dot_general | solution.py:417
  21.6 0.7 multiply_convert_fusion
  22.3 0.1 multiply_reduce_fusion.1
  22.4 0.1 fusion.7
  22.6 0.1 multiply_convert_fusion.1
  22.7 0.1 pad_maximum_fusion.1
  22.7 0.7 concatenate.30.kv_in
  23.5 33.5 %latent_gather.1 = (bf16[4,4,4,2,16,1152]{5,4,3,2,1,0:T(8,128)(2,1)}, bf16[2,4,2,16,1536]{4,3,2,1,0:T(8,128)(2,1)}, f32[2,4,2,16,128]{4,3,2,1,0:T(8,128)}) custom-call(bf16[16,1152]{1,0:T(8,128)(2,1)} %concatenate.30.kv_in, bf16[2,16,1536]{2,1,0:T(8,128)(2,1)} %bitcast.14, f32[2,16,128]{2,1,0:T(8,128)} %pad_maximum_fusion.tab_in), custom_call_target="tpu_custom_call" | custom-call | tf_op jit(solution)/shard_map/latent_gather/pallas_call | solution.py:149
  57.0 40.1 %latent_attention.1 = bf16[256,2048]{1,0:T(8,128)(2,1)} custom-call(bf16[256,1536]{1,0:T(8,128)(2,1)} %bitcast.13, f32[256,128]{1,0:T(8,128)} %bitcast.15, bf16[2048,1152]{1,0:T(8,128)(2,1)} %bitcast.11, bf16[1536,24576]{1,0:T(8,128)(2,1)} %wq_hbm.1, bf16[512,32768]{1,0:T(8,128)(2,1)} %wkv_hbm.1), custom_call_target="tpu_custom_call" | custom-call | tf_op jit(solution)/shard_map/latent_attention/pallas_call | solution.py:260
  97.1 39.8 %out_projection.1 = (bf16[16,7168]{1,0:T(8,128)(2,1)}, bf16[16,7168]{1,0:T(8,128)(2,1)}) custom-call(bf16[2,4,2,16,2048]{4,3,2,1,0:T(8,128)(2,1)} %bitcast.12, bf16[16384,7168]{1,0:T(8,128)(2,1)} %w_hbm.1), custom_call_target="tpu_custom_call" | custom-call | tf_op jit(solution)/shard_map/out_projection/pallas_call | solution.py:391
  136.8 1.6 %copy.16 = bf16[16,7168]{1,0:T(8,128)(2,1)} copy(bf16[16,7168]{1,0:T(8,128)(2,1)} %get-tuple-element.20) | data formatting | bytes 458752
  138.5 1.6 %copy.17 = bf16[16,7168]{1,0:T(8,128)(2,1)} copy(bf16[16,7168]{1,0:T(8,128)(2,1)} %get-tuple-element.21) | data formatting | bytes 458752
  (4 shorter events, 0.0 us)

commit v2 on v0

v2 whole, which is shorter than its diff:
```python
import numpy as np
import jax
import jax.numpy as jnp
from jax import lax
from jax.experimental import pallas as pl
from jax.experimental.pallas import tpu as pltpu
from jax.sharding import PartitionSpec as P

D_MODEL = 7168
HEADS = 128
Q_LAT = 1536
KV_LAT = 512
ROPE_DIM = 64
NOPE_DIM = 128
V_DIM = 128
QK_DIM = NOPE_DIM + ROPE_DIM
KV_DOWN = KV_LAT + ROPE_DIM
ROPE_BASE = 10000.0
NORM_EPS = 1e-6

ROWS = 16
RING = 4
GROUP = 2 * RING
G_HEADS = HEADS // GROUP
TOKENS = 2048
KV_W = 2 * KV_LAT + 2 * ROPE_DIM
Q_W = KV_LAT + 2 * ROPE_DIM
UNIT = 2 * ROWS
G_ROWS = 2 * RING * UNIT
HALF_N = D_MODEL // 2
OUT_ROWS = 2 * UNIT
K_COLS = G_HEADS * V_DIM
MESH = pl.DeviceIdType.MESH

COLORS = (((0, 256), (2, 1, 0)), ((256, 640), (1, 0, 2)), ((640, 1152), (0, 2, 1)))

W_ROWS = 512
W_SLOTS = 8
N_DOWN = D_MODEL // W_ROWS
N_UP = Q_LAT // W_ROWS
N_OUT = HEADS * V_DIM // W_ROWS
FIRST_OUT = N_DOWN + N_UP
N_CHUNKS = FIRST_OUT + N_OUT
PER_RANK = K_COLS // W_ROWS
KV_SLOTS = 4

ORDER = ((0, 0), (0, 1), (1, 0), (3, 0), (1, 1), (2, 0), (3, 1), (2, 1))


def coords():
    me = lax.axis_index("sp")
    return me // 32, lax.rem(me // 8, 4), lax.rem(me // 2, 4), lax.rem(me, 2)


def device(z, y, x, c):
    return {"sp": ((z * RING + y) * RING + x) * 2 + c}


def shifted(pos, axis, k):
    out = list(pos)
    out[axis] = lax.rem(pos[axis] + k, RING)
    return tuple(out)


def block_kernel(x_one, x_two, gain_q, gain_kv, tab_in, wqd, wkvd, wqu, wkvu, wout, y_one, y_two,
                 xs, qd, kd, kvd_buf, w_buf, wkv, kv_ref, q_ref, tab_ref, q_eff, o_ref, o_all, acc, y_send,
                 w_sem, kvd_sem, wkv_sem, kv_send, kv_recv, r_send, r_recv, d_send, d_recv,
                 q_send, q_recv, t_send, t_recv, dq_send, dq_recv, a_send, a_recv, p_send, p_recv, y_ssem, y_rsem):
    z, y, x, c = coords()
    pos = (z, y, x)
    rank = z * 2 + c
    other = device(z, y, x, 1 - c)
    trans = (((1,), (1,)), ((), ()))

    def rank_at(j):
        out = jnp.int32(0)
        for i, (k, flip) in enumerate(ORDER):
            cc = c if flip == 0 else 1 - c
            out = jnp.where(j == i, lax.rem(z + RING - k, RING) * 2 + cc, out)
        return out

    def down_copy(s):
        slot = lax.rem(s, W_SLOTS)
        return pltpu.make_async_copy(
            wqd.at[pl.ds(pl.multiple_of(s * W_ROWS, W_ROWS), W_ROWS), :], w_buf.at[slot, :, pl.ds(0, Q_LAT)], w_sem.at[slot])

    def up_copy(s):
        slot = lax.rem(s, W_SLOTS)
        width = G_HEADS * QK_DIM
        return pltpu.make_async_copy(
            wqu.at[pl.ds(pl.multiple_of((s - N_DOWN) * W_ROWS, W_ROWS), W_ROWS), pl.ds(pl.multiple_of(rank * width, 128), width)],
            w_buf.at[slot, :, pl.ds(0, width)], w_sem.at[slot])

    def out_copy(s):
        slot = lax.rem(s, W_SLOTS)
        t = s - FIRST_OUT
        row = pl.multiple_of(rank_at(t // PER_RANK) * K_COLS + lax.rem(t, PER_RANK) * W_ROWS, W_ROWS)
        return pltpu.make_async_copy(
            wout.at[pl.ds(row, W_ROWS), pl.ds(pl.multiple_of(c * HALF_N, 128), HALF_N)], w_buf.at[slot], w_sem.at[slot])

    def kvd_copy(s):
        slot = lax.rem(s, KV_SLOTS)
        return pltpu.make_async_copy(
            wkvd.at[:, pl.ds(pl.multiple_of(s * W_ROWS, W_ROWS), W_ROWS)], kvd_buf.at[slot], kvd_sem.at[slot])

    wkv_copy = pltpu.make_async_copy(
        wkvu.at[:, pl.ds(pl.multiple_of(rank * (G_HEADS * 256), 128), G_HEADS * 256)], wkv, wkv_sem)

    for s in range(W_SLOTS):
        down_copy(jnp.int32(s)).start()
        if s < KV_SLOTS:
            kvd_copy(jnp.int32(s)).start()

    barrier = pltpu.get_barrier_semaphore()
    for axis in range(3):
        for k in range(1, RING):
            pl.semaphore_signal(barrier, inc=1, device_id=device(*shifted(pos, axis, k), c), device_id_type=MESH)
    pl.semaphore_signal(barrier, inc=1, device_id=other, device_id_type=MESH)

    xs[:ROWS] = x_one[...]
    xs[ROWS:] = x_two[...]
    tab_ref[:, z, c] = tab_in[...]
    qd[...] = jnp.zeros_like(qd)
    kd[...] = jnp.zeros_like(kd)

    @pl.loop(0, N_DOWN)
    def _(i):
        lhs = xs[:, pl.ds(pl.multiple_of(i * W_ROWS, W_ROWS), W_ROWS)]
        kvd_copy(i).wait()
        kd[:, :KV_DOWN] += lax.dot_general(lhs, kvd_buf[lax.rem(i, KV_SLOTS)], trans, preferred_element_type=jnp.float32)
        down_copy(i).wait()
        qd[...] += jnp.dot(lhs, w_buf[lax.rem(i, W_SLOTS), :, :Q_LAT], preferred_element_type=jnp.float32)

        @pl.when(i + KV_SLOTS < N_DOWN)
        def _():
            kvd_copy(i + KV_SLOTS).start()

        @pl.when(i + W_SLOTS < N_DOWN)
        def _():
            down_copy(i + W_SLOTS).start()

    for s in range(N_DOWN, N_DOWN + W_SLOTS):
        if s < FIRST_OUT:
            up_copy(jnp.int32(s)).start()
        if s == FIRST_OUT:
            wkv_copy.start()
        if s >= FIRST_OUT:
            out_copy(jnp.int32(s)).start()

    lane16 = lax.broadcasted_iota(jnp.int32, (ROWS, 128), 1)
    t0, t1 = tab_in[0], tab_in[1]
    cos2 = jnp.where(lane16 < 32, t0, jnp.where(lane16 < 64, pltpu.roll(t0, 32, 1), jnp.where(lane16 < 96, pltpu.roll(t1, 64, 1), pltpu.roll(t1, 96, 1))))
    sin_hi = jnp.where((lane16 >= 32) & (lane16 < 64), t0, jnp.where(lane16 >= 96, pltpu.roll(t1, 64, 1), 0.0))
    sin_lo = jnp.where(lane16 < 32, -pltpu.roll(t0, 96, 1), jnp.where((lane16 >= 64) & (lane16 < 96), -pltpu.roll(t1, 32, 1), 0.0))
    u = kd[:, :KV_LAT]
    lat = (u * lax.rsqrt(jnp.mean(u * u, axis=-1, keepdims=True) + NORM_EPS) * gain_kv[...]).astype(jnp.bfloat16)
    kv_ref[z, y, x, c, :, 0:KV_LAT] = lat[:ROWS]
    kv_ref[z, y, x, c, :, KV_LAT:2 * KV_LAT] = lat[ROWS:]
    rot = jnp.where(lane16 < 64, kd[:ROWS, KV_LAT:], pltpu.roll(kd[ROWS:, KV_LAT:], 64, 1))
    rot = rot * cos2 + pltpu.roll(rot, 32, 1) * sin_hi + pltpu.roll(rot, 96, 1) * sin_lo
    kv_ref[z, y, x, c, :, 2 * KV_LAT:] = rot.astype(jnp.bfloat16)
    v = qd[...]
    q_lat = (v * lax.rsqrt(jnp.mean(v * v, axis=-1, keepdims=True) + NORM_EPS) * gain_q[...]).astype(jnp.bfloat16)
    q_ref[:, z, c] = q_lat.reshape(2, ROWS, Q_LAT)
    pl.semaphore_wait(barrier, 10)

    def kv_piece(color, phase, at, core, half=None):
        (lo, hi), order = COLORS[color]
        index = [at[0], at[1], at[2]]
        for axis in order[:phase]:
            index[axis] = slice(None)
        if half is not None:
            index[order[0]] = pl.ds(2 * half, 2)
        return kv_ref.at[index[0], index[1], index[2], core, :, pl.ds(lo, hi - lo)]

    def remote(piece, send, recv, to):
        return pltpu.make_async_remote_copy(
            src_ref=piece, dst_ref=piece, send_sem=send, recv_sem=recv, device_id=to, device_id_type=MESH)

    def kv_copy(color, phase, k, at, to):
        return remote(kv_piece(color, phase, at, c), kv_send.at[color, phase, k - 1], kv_recv.at[color, phase, k - 1], to)

    def relay_copy(color, half, at, to):
        return remote(kv_piece(color, 2, at, c, half), r_send.at[color, half], r_recv.at[color, half], to)

    def pass_copy(color, k, at, core):
        return remote(kv_piece(color, 2, at, core), d_send.at[color, k], d_recv.at[color, k], other)

    def q_copy(zz, cc, to, send, recv):
        return remote(q_ref.at[:, zz, cc], send, recv, to)

    def t_copy(zz, cc, to, send, recv):
        return remote(tab_ref.at[:, zz, cc], send, recv, to)

    def start_phase(phase):
        for color in range(3):
            axis = COLORS[color][1][phase]
            for k in (1, 3, 2) if phase < 2 else (1, 3):
                kv_copy(color, phase, k, pos, device(*shifted(pos, axis, k), c)).start()

    def wait_phase(phase):
        for k in (1, 3, 2):
            for color in range(3):
                kv_copy(color, phase, k, shifted(pos, COLORS[color][1][phase], RING - k), other).wait_recv()

    start_phase(0)
    for k in (1, 3, 2):
        to = device(*shifted(pos, 0, k), c)
        t_copy(z, c, to, t_send.at[k - 1], t_recv.at[k - 1]).start()
        q_copy(z, c, to, q_send.at[k - 1], q_recv.at[k - 1]).start()
    t_copy(z, c, other, dq_send.at[0, 0], dq_recv.at[0, 0]).start()
    q_copy(z, c, other, dq_send.at[1, 0], dq_recv.at[1, 0]).start()
    wait_phase(0)
    start_phase(1)
    for k in (1, 3, 2):
        zz = lax.rem(z + RING - k, RING)
        t_copy(zz, c, other, t_send.at[k - 1], t_recv.at[k - 1]).wait_recv()
        t_copy(zz, c, other, dq_send.at[0, k], dq_recv.at[0, k]).start()
        q_copy(zz, c, other, q_send.at[k - 1], q_recv.at[k - 1]).wait_recv()
        q_copy(zz, c, other, dq_send.at[1, k], dq_recv.at[1, k]).start()
    wait_phase(1)
    start_phase(2)
    for color in range(3):
        pass_copy(color, 0, pos, c).start()
    for k in range(RING):
        zz = lax.rem(z + RING - k, RING)
        t_copy(zz, 1 - c, other, dq_send.at[0, k], dq_recv.at[0, k]).wait()
        q_copy(zz, 1 - c, other, dq_send.at[1, k], dq_recv.at[1, k]).wait()

    q2 = q_ref.reshape(G_ROWS, Q_LAT)
    tab2 = tab_ref.reshape(G_ROWS, 128)
    kv2 = kv_ref.reshape(TOKENS, KV_W)
    lane = lax.broadcasted_iota(jnp.int32, (G_ROWS, 128), 1)
    tab = tab2[...]
    cos_t = jnp.where(lane < 32, tab, jnp.where(lane < 64, pltpu.roll(tab, 32, 1), 0.0))
    sin_b = jnp.where((lane >= 32) & (lane < 64), tab, 0.0)
    sin_a = jnp.where(lane < 32, -pltpu.roll(tab, 96, 1), 0.0)

    def put_rope(head, part):
        out = part * cos_t + pltpu.roll(part, 32, 1) * sin_b + pltpu.roll(part, 96, 1) * sin_a
        half = G_ROWS // 2
        out = jnp.concatenate([out[:half], pltpu.roll(out[half:], 64, 1)], axis=0)
        q_eff[:, :, head, :, KV_LAT:] = out.astype(jnp.bfloat16).reshape(2, RING, UNIT, 128)

    def put_nope(head, part):
        w_k = wkv[:, pl.ds(pl.multiple_of(head * 256, 256), 128)]
        out = lax.dot_general(part.astype(jnp.bfloat16), w_k, (((1,), (1,)), ((), ())), preferred_element_type=jnp.float32)
        q_eff[:, :, head, :, :KV_LAT] = out.astype(jnp.bfloat16).reshape(2, RING, UNIT, KV_LAT)

    for s in range(N_DOWN, FIRST_OUT):
        up_copy(jnp.int32(s)).wait()
    wkv_copy.wait()

    def queries(lo, hi):
        @pl.loop(lo, hi)
        def _(p):
            cols = pl.ds(pl.multiple_of(p * (2 * QK_DIM), 128), 2 * QK_DIM)
            f = jnp.zeros((G_ROWS, 2 * QK_DIM), jnp.float32)
            for i in range(N_UP):
                f = f + jnp.dot(q2[:, i * W_ROWS:(i + 1) * W_ROWS], w_buf[(N_DOWN + i) % W_SLOTS, :, cols],
                                preferred_element_type=jnp.float32)
            head = p * 2
            put_nope(head, f[:, :128])
            put_rope(head, f[:, 128:256])
            mid = pltpu.roll(f[:, 128:256], 64, 1)
            last = pltpu.roll(f[:, 256:384], 64, 1)
            put_nope(head + 1, jnp.where(lane < 64, mid, last))
            put_rope(head + 1, last)

    queries(0, G_HEADS // 2)
    for s in range(N_DOWN + W_SLOTS, FIRST_OUT + W_SLOTS):
        out_copy(jnp.int32(s)).start()

    for k in (1, 3):
        for color in range(3):
            axis = COLORS[color][1][2]
            source = shifted(pos, axis, RING - k)
            kv_copy(color, 2, k, source, other).wait_recv()
            relay_copy(color, k // 2, source, device(*shifted(pos, axis, k), c)).start()
            pass_copy(color, k, source, c).start()
    for color in range(3):
        source = shifted(pos, COLORS[color][1][2], 2)
        for half in range(2):
            relay_copy(color, half, source, other).wait_recv()
        pass_copy(color, 2, source, c).start()
    for k in (0, 1, 3, 2):
        for color in range(3):
            pass_copy(color, k, shifted(pos, COLORS[color][1][2], RING - k), 1 - c).wait_recv()

    def ring_copy(mb, k, zz, src_rank, to):
        return pltpu.make_async_remote_copy(
            src_ref=o_ref.at[mb, zz], dst_ref=o_all.at[src_rank, mb], send_sem=a_send.at[mb, k - 1],
            recv_sem=a_recv.at[mb, k - 1], device_id=to, device_id_type=MESH)

    def pair_copy(mb, k, src_rank, src):
        return pltpu.make_async_remote_copy(
            src_ref=src, dst_ref=o_all.at[src_rank, mb], send_sem=p_send.at[mb, k], recv_sem=p_recv.at[mb, k],
            device_id=other, device_id_type=MESH)

    scale2 = (QK_DIM ** -0.5) * 1.4426950408889634
    tok = lax.broadcasted_iota(jnp.int32, (UNIT, 1), 0)

    @pl.loop(0, 2)
    def _(mb):
        lat_cols = pl.ds(pl.multiple_of(mb * KV_LAT, KV_LAT), KV_LAT)
        for zz in range(RING):
            length = (zz + 1) * 512
            key = lax.broadcasted_iota(jnp.int32, (UNIT, length), 1)
            q_tok = zz * 512 + y * 128 + x * 32 + tok
            p0 = tab2[pl.ds(pl.multiple_of((mb * RING + zz) * UNIT, UNIT), UNIT), 64:65].astype(jnp.int32)
            cap = jnp.where((key <= q_tok) & (key >= q_tok - p0), 3e38, -1e30).astype(jnp.float32)
            q = q_eff[mb, zz].reshape(G_HEADS * UNIT, Q_W)
            keys = kv2[:length, lat_cols]
            s = lax.dot_general(q[:, :KV_LAT], keys, trans, preferred_element_type=jnp.float32)
            s = s + lax.dot_general(q[:, KV_LAT:], kv2[:length, 2 * KV_LAT:], trans, preferred_element_type=jnp.float32)
            s = jnp.minimum(s.reshape(G_HEADS, UNIT, length), cap[None])
            top = jnp.max(s, axis=-1, keepdims=True)
            e = jnp.exp2((s - top) * scale2)
            total = jnp.sum(e, axis=-1, keepdims=True)
            e = e.astype(jnp.bfloat16).reshape(G_HEADS * UNIT, length)
            o = jnp.dot(e, keys, preferred_element_type=jnp.float32).reshape(G_HEADS, UNIT, KV_LAT)
            q_eff[mb, zz, :, :, :KV_LAT] = (o / total).astype(jnp.bfloat16)

        @pl.loop(0, G_HEADS)
        def _(h):
            w_v = wkv[:, pl.ds(pl.multiple_of(h * 256 + 128, 128), 128)]
            o_h = jnp.dot(q_eff[mb, :, h, :, :KV_LAT].reshape(RING * UNIT, KV_LAT), w_v, preferred_element_type=jnp.float32)
            o_ref[mb, :, :, :, pl.ds(pl.multiple_of(h * 128, 128), 128)] = o_h.astype(jnp.bfloat16).reshape(RING, 2, ROWS, V_DIM)

        for k in (1, 3, 2):
            zz = lax.rem(z + k, RING)
            ring_copy(mb, k, zz, rank, device(zz, y, x, c)).start()
        pair_copy(mb, 0, rank, o_ref.at[mb, z]).start()

    o_all[rank] = o_ref[:, z]
    acc[...] = jnp.zeros_like(acc)

    @pl.loop(0, N_OUT)
    def _(t):
        for i, (k, flip) in enumerate(ORDER):
            if i == 0:
                continue

            @pl.when(t == i * PER_RANK)
            def _(i=i, k=k, flip=flip):
                src_rank = lax.rem(z + RING - k, RING) * 2 + (c if flip == 0 else 1 - c)
                for mb in range(2):
                    if flip == 0:
                        ring_copy(mb, k, z, src_rank, other).wait_recv()
                        pair_copy(mb, k, src_rank, o_all.at[src_rank, mb]).start()
                    else:
                        pair_copy(mb, k, src_rank, o_all.at[src_rank, mb]).wait_recv()

        s = t + FIRST_OUT
        cols = pl.ds(pl.multiple_of(lax.rem(t, PER_RANK) * W_ROWS, W_ROWS), W_ROWS)
        lhs = o_all[rank_at(t // PER_RANK), :, :, :, cols].reshape(OUT_ROWS, W_ROWS)
        out_copy(s).wait()
        slot = lax.rem(s, W_SLOTS)
        step_n = 512
        for n in range(HALF_N // step_n):
            part = slice(n * step_n, (n + 1) * step_n)
            acc[:, part] += jnp.dot(lhs, w_buf[slot, :, part], preferred_element_type=jnp.float32)

        @pl.when(s + W_SLOTS < N_CHUNKS)
        def _():
            out_copy(s + W_SLOTS).start()

    acc4 = acc.reshape(2, 2, ROWS, HALF_N)
    my_cols = pl.ds(pl.multiple_of(c * HALF_N, 128), HALF_N)
    their_cols = pl.ds(pl.multiple_of((1 - c) * HALF_N, 128), HALF_N)
    outs = (y_one, y_two)

    def y_copy(mb, cols):
        return pltpu.make_async_remote_copy(
            src_ref=y_send.at[mb], dst_ref=outs[mb].at[:, cols], send_sem=y_ssem.at[mb], recv_sem=y_rsem.at[mb],
            device_id=other, device_id_type=MESH)

    for mb in range(2):
        y_send[mb] = acc4[mb, 1 - c].astype(jnp.bfloat16)
    for mb in range(2):
        outs[mb][:, my_cols] = acc4[mb, c].astype(jnp.bfloat16)
    for mb in range(2):
        y_copy(mb, my_cols).start()

    for k in range(1, RING):
        t_copy(z, c, other, t_send.at[k - 1], t_recv.at[k - 1]).wait_send()
        q_copy(z, c, other, q_send.at[k - 1], q_recv.at[k - 1]).wait_send()
        for color in range(3):
            for phase in range(3):
                if phase < 2 or k != 2:
                    kv_copy(color, phase, k, pos, other).wait_send()
    for color in range(3):
        for half in range(2):
            relay_copy(color, half, pos, other).wait_send()
        for k in range(RING):
            pass_copy(color, k, pos, c).wait_send()
    for mb in range(2):
        for k in range(1, RING):
            ring_copy(mb, k, z, rank, other).wait_send()
        for k in range(RING):
            pair_copy(mb, k, rank, o_all.at[rank, mb]).wait_send()
        y_copy(mb, their_cols).wait()


def block(x_one, x_two, gain_q, gain_kv, tab, w_qdown, w_kvdown, w_qup, w_kvup, w_out):
    dma = pltpu.SemaphoreType.DMA
    vmem = pl.BlockSpec(memory_space=pltpu.VMEM)
    hbm = pl.BlockSpec(memory_space=pl.ANY)
    y_shape = jax.ShapeDtypeStruct((ROWS, D_MODEL), jnp.bfloat16)
    bf, f32 = jnp.bfloat16, jnp.float32
    return pl.pallas_call(
        block_kernel,
        out_shape=(y_shape, y_shape),
        in_specs=[vmem] * 5 + [hbm] * 5,
        out_specs=(vmem, vmem),
        scratch_shapes=[
            pltpu.VMEM((2 * ROWS, D_MODEL), bf),
            pltpu.VMEM((2 * ROWS, Q_LAT), f32),
            pltpu.VMEM((2 * ROWS, KV_LAT + 128), f32),
            pltpu.VMEM((KV_SLOTS, KV_DOWN, W_ROWS), bf),
            pltpu.VMEM((W_SLOTS, W_ROWS, HALF_N), bf),
            pltpu.VMEM((KV_LAT, G_HEADS * 256), bf),
            pltpu.VMEM((RING, RING, RING, 2, ROWS, KV_W), bf),
            pltpu.VMEM((2, RING, 2, ROWS, Q_LAT), bf),
            pltpu.VMEM((2, RING, 2, ROWS, 128), f32),
            pltpu.VMEM((2, RING, G_HEADS, UNIT, Q_W), bf),
            pltpu.VMEM((2, RING, 2, ROWS, K_COLS), bf),
            pltpu.VMEM((GROUP, 2, 2, ROWS, K_COLS), bf),
            pltpu.VMEM((OUT_ROWS, HALF_N), f32),
            pltpu.VMEM((2, ROWS, HALF_N), bf),
            dma((W_SLOTS,)), dma((KV_SLOTS,)), dma,
            dma((3, 3, 3)), dma((3, 3, 3)), dma((3, 2)), dma((3, 2)), dma((3, 4)), dma((3, 4)),
            dma((3,)), dma((3,)), dma((3,)), dma((3,)), dma((2, 4)), dma((2, 4)),
            dma((2, 3)), dma((2, 3)), dma((2, 4)), dma((2, 4)), dma((2,)), dma((2,)),
        ],
        compiler_params=pltpu.CompilerParams(collective_id=0, has_side_effects=True, vmem_limit_bytes=67043328),
        name="latent_attention_block",
    )(x_one, x_two, gain_q, gain_kv, tab, w_qdown, w_kvdown, w_qup, w_kvup, w_out)


def tables(pos_one, pos_two):
    lane = np.arange(128)
    inv_freq = (ROPE_BASE ** (-(lane % 32) / (ROPE_DIM // 2))).astype(np.float32)
    pos = jnp.stack([pos_one, pos_two]).astype(jnp.float32)[:, :, None]
    angles = pos * inv_freq
    return jnp.where(lane < 32, jnp.cos(angles), jnp.where(lane < 64, jnp.sin(angles), pos))


def solution(mesh):
    tok_spec = P(('dp', 'sp'), None)
    idx_spec = P(('dp', 'sp'))

    def local_body(x_one, seg_one, pos_one, x_two, seg_two, pos_two, w_qdown, gain_q, w_qup, w_kvdown, gain_kv, w_kvup, w_out):
        gains = (gain_q.astype(jnp.float32)[None], gain_kv.astype(jnp.float32)[None])
        return block(x_one, x_two, *gains, tables(pos_one, pos_two), w_qdown, w_kvdown.T, w_qup, w_kvup, w_out)

    return jax.shard_map(local_body, mesh=mesh, in_specs=(tok_spec, idx_spec, idx_spec, tok_spec, idx_spec, idx_spec, P(), P(), P(), P(), P(), P(), P()), out_specs=(tok_spec, tok_spec), check_vma=False)
```

time: 551 us -> 106 us (0.19); the launches traced: 543 us -> 105 us
  matrix products: 229 us -> 0 us
  blocking collectives: 138 us -> 0 us
  waiting for transfers between devices: 116 us -> 0 us
  Pallas kernels: 0 us -> 96.8 us
  other arithmetic: 24 us -> 3.39 us
  starting transfers between devices: 15.9 us -> 0 us
  between operations: 14.5 us -> 0.64 us
    dot_general x16 -> x0, matrix products: 229 us -> none  [the longest x2 144 us: micro_block(): jnp.dot(attn_flat, w_out, preferred_element_type=jnp.float32)]
    all_gather x4 -> x0, waiting for transfers between devices: 102 us -> none  [the longest x2 102 us: micro_block(): q_all = lax.all_gather(q_latent, 'sp', axis=0, tiled=True)]
    pallas_call x0 -> x1, Pallas kernels: none -> 96.8 us  [block(): pl.pallas_call(block_kernel, out_shape=(y_shape, y_shape), in_specs=[vmem...]
    unnamed x1 -> x0, blocking collectives: 69.7 us -> none
    all_gather x2 -> x0, blocking collectives: 68.5 us -> none  [micro_block(): rope_all = lax.all_gather(k_rope, 'sp', axis=0, tiled=True)]
    reduce_sum x4 -> x0, other arithmetic: 16.5 us -> none  [the longest x2 16.2 us: head_attention(): jax.nn.softmax(jnp.where(allowed[None], scores * QK_DIM ** (-0.5), -1e+30...]
    all_to_all x2 -> x0, starting transfers between devices: 15.8 us -> none  [micro_block(): tok_out = lax.all_to_all(head_out, 'sp', 0, 1, tiled=True)]
    all_to_all x2 -> x0, waiting for transfers between devices: 12.6 us -> none  [micro_block(): tok_out = lax.all_to_all(head_out, 'sp', 0, 1, tiled=True)]
  transfers between devices with their start and end apart: 6 -> 0, of which waited for: 3 -> 0; matrix products, arithmetic and copies ran while one was open for 11% -> 0% of each run, Pallas kernels for 0% -> 0%
where the time goes in v2:
time: 106 us; the launch traced here: 105 us
  Pallas kernels  96.8 us (91%)
  local copies, waits for them, and re-layouts  4.56 us (4%)
  other arithmetic  3.39 us (3%)
    pallas_call x1, Pallas kernels, block(): pl.pallas_call(block_kernel, out_shape=(y_shape, y_shape), in_specs=[vmem...  96.8 us
    unnamed x2, local copies, waits for them, and re-layouts  3.28 us

profile of v2, /device:TPU:1, one launch (start us, length us, event | category | flops | bytes accessed | tf_op | source)
XLA Modules:
  0.0 105.4 jit_solution(10631460723275072588)
XLA Ops:
  0.6 0.7 add_convert_fusion
  1.3 1.3 %broadcast_in_dim.33 = f32[512]{0:T(512)} convert(bf16[512]{0:T(512)(128)(2,1)} %param.24) | non-fusion elementwise | flops 512 | bytes 3072 | tf_op jit(solution)/shard_map/broadcast_in_dim | solution.py:454
  2.6 1.3 %reshape.22.gain_q = f32[1,1536]{1,0:T(1,128)} reshape(bf16[1536]{0:T(1024)(128)(2,1)} %param.21) | data formatting | bytes 9216 | tf_op jit(solution)/shard_map/broadcast_in_dim | solution.py:454
  3.9 1.4 %fusion.tab_in = f32[2,16,128]{2,1,0:T(8,128)} fusion(f32[128]{0:T(128)} %constant.6.clone, f32[2,16]{1,0:T(2,128)S(1)} %add_convert_fusion, pred[128]{0:T(512)(128)(4,1)} %constant.7.clone, pred[128]{0:T(512)(128)(4,1)} %constant.8.clone), kind=kLoop, calls=%fused_computation.2 | loop fusion | flops 12288 | bytes 17280 | tf_op jit(solution)/shard_map/jit(_where)/select_n | solution.py:446
  5.3 96.8 %latent_attention_block.1 = (bf16[16,7168]{1,0:T(8,128)(2,1)}, bf16[16,7168]{1,0:T(8,128)(2,1)}) custom-call(bf16[16,7168]{1,0:T(8,128)(2,1)} %x_one.1, bf16[16,7168]{1,0:T(8,128)(2,1)} %x_two.1, f32[1,1536]{1,0:T(1,128)} %reshape.22.gain_q, f32[1,512]{1,0:T(1,128)} %bitcast.5, f32[2,16,128]{2,1,0:T(8,128)} %fusion.tab_in, bf16[7168,1536]{1,0:T(8,128)(2,1)} %wqd.1, ...), custom_call_target="tpu_custom_call" | custom-call | tf_op jit(solution)/shard_map/latent_attention_block/pallas_call | solution.py:411
  102.1 1.6 %copy.18 = bf16[16,7168]{1,0:T(8,128)(2,1)} copy(bf16[16,7168]{1,0:T(8,128)(2,1)} %get-tuple-element.4) | data formatting | bytes 458752
  103.8 1.6 %copy.19 = bf16[16,7168]{1,0:T(8,128)(2,1)} copy(bf16[16,7168]{1,0:T(8,128)(2,1)} %get-tuple-element.5) | data formatting | bytes 458752

commit v3 on v2

--- a/solution.py
+++ b/solution.py
@@ -1,4 +1,3 @@
-import numpy as np
 import jax
 import jax.numpy as jnp
 from jax import lax
@@ -36,13 +35,14 @@
 
 W_ROWS = 512
 W_SLOTS = 8
+N_KV = 2
 N_DOWN = D_MODEL // W_ROWS
 N_UP = Q_LAT // W_ROWS
 N_OUT = HEADS * V_DIM // W_ROWS
-FIRST_OUT = N_DOWN + N_UP
+FIRST_UP = N_KV + N_DOWN
+FIRST_OUT = FIRST_UP + N_UP
 N_CHUNKS = FIRST_OUT + N_OUT
 PER_RANK = K_COLS // W_ROWS
-KV_SLOTS = 4
 
 ORDER = ((0, 0), (0, 1), (1, 0), (3, 0), (1, 1), (2, 0), (3, 1), (2, 1))
 
@@ -62,9 +62,9 @@
     return tuple(out)
 
 
-def block_kernel(x_one, x_two, gain_q, gain_kv, tab_in, wqd, wkvd, wqu, wkvu, wout, y_one, y_two,
-                 xs, qd, kd, kvd_buf, w_buf, wkv, kv_ref, q_ref, tab_ref, q_eff, o_ref, o_all, acc, y_send,
-                 w_sem, kvd_sem, wkv_sem, kv_send, kv_recv, r_send, r_recv, d_send, d_recv,
+def block_kernel(pos_one, pos_two, gain_q, gain_kv, x_one, x_two, wqd, wkvd, wqu, wkvu, wout, y_ref,
+                 xs, qd, kd, kr_buf, w_buf, wkv, kv_ref, q_ref, tab_ref, q_eff, o_ref, o_all, acc, y_send,
+                 x_sem, w_sem, kr_sem, wkv_sem, kv_send, kv_recv, r_send, r_recv, d_send, d_recv,
                  q_send, q_recv, t_send, t_recv, dq_send, dq_recv, a_send, a_recv, p_send, p_recv, y_ssem, y_rsem):
     z, y, x, c = coords()
     pos = (z, y, x)
@@ -79,16 +79,26 @@
             out = jnp.where(j == i, lax.rem(z + RING - k, RING) * 2 + cc, out)
         return out
 
+    def x_copy(i):
+        return pltpu.make_async_copy((x_one, x_two)[i], xs.at[pl.ds(i * ROWS, ROWS), :], x_sem.at[i])
+
+    def lat_copy(s):
+        return pltpu.make_async_copy(wkvd.at[pl.ds(0, KV_LAT), pl.ds(s * HALF_N, HALF_N)], w_buf.at[s], w_sem.at[s])
+
+    def kr_copy(s):
+        return pltpu.make_async_copy(
+            wkvd.at[pl.ds(KV_LAT, ROPE_DIM), pl.ds(s * HALF_N, HALF_N)], kr_buf.at[s], kr_sem.at[s])
+
     def down_copy(s):
         slot = lax.rem(s, W_SLOTS)
         return pltpu.make_async_copy(
-            wqd.at[pl.ds(pl.multiple_of(s * W_ROWS, W_ROWS), W_ROWS), :], w_buf.at[slot, :, pl.ds(0, Q_LAT)], w_sem.at[slot])
+            wqd.at[pl.ds(pl.multiple_of((s - N_KV) * W_ROWS, W_ROWS), W_ROWS), :], w_buf.at[slot, :, pl.ds(0, Q_LAT)], w_sem.at[slot])
 
     def up_copy(s):
         slot = lax.rem(s, W_SLOTS)
         width = G_HEADS * QK_DIM
         return pltpu.make_async_copy(
-            wqu.at[pl.ds(pl.multiple_of((s - N_DOWN) * W_ROWS, W_ROWS), W_ROWS), pl.ds(pl.multiple_of(rank * width, 128), width)],
+            wqu.at[pl.ds(pl.multiple_of((s - FIRST_UP) * W_ROWS, W_ROWS), W_ROWS), pl.ds(pl.multiple_of(rank * width, 128), width)],
             w_buf.at[slot, :, pl.ds(0, width)], w_sem.at[slot])
 
     def out_copy(s):
@@ -98,18 +108,16 @@
         return pltpu.make_async_copy(
             wout.at[pl.ds(row, W_ROWS), pl.ds(pl.multiple_of(c * HALF_N, 128), HALF_N)], w_buf.at[slot], w_sem.at[slot])
 
-    def kvd_copy(s):
-        slot = lax.rem(s, KV_SLOTS)
-        return pltpu.make_async_copy(
-            wkvd.at[:, pl.ds(pl.multiple_of(s * W_ROWS, W_ROWS), W_ROWS)], kvd_buf.at[slot], kvd_sem.at[slot])
-
     wkv_copy = pltpu.make_async_copy(
         wkvu.at[:, pl.ds(pl.multiple_of(rank * (G_HEADS * 256), 128), G_HEADS * 256)], wkv, wkv_sem)
 
-    for s in range(W_SLOTS):
+    for i in range(2):
+        x_copy(i).start()
+    for s in range(N_KV):
+        lat_copy(s).start()
+        kr_copy(s).start()
+    for s in range(N_KV, W_SLOTS):
         down_copy(jnp.int32(s)).start()
-        if s < KV_SLOTS:
-            kvd_copy(jnp.int32(s)).start()
 
     barrier = pltpu.get_barrier_semaphore()
     for axis in range(3):
@@ -117,52 +125,56 @@
             pl.semaphore_signal(barrier, inc=1, device_id=device(*shifted(pos, axis, k), c), device_id_type=MESH)
     pl.semaphore_signal(barrier, inc=1, device_id=other, device_id_type=MESH)
 
-    xs[:ROWS] = x_one[...]
-    xs[ROWS:] = x_two[...]
-    tab_ref[:, z, c] = tab_in[...]
-    qd[...] = jnp.zeros_like(qd)
-    kd[...] = jnp.zeros_like(kd)
-
-    @pl.loop(0, N_DOWN)
-    def _(i):
-        lhs = xs[:, pl.ds(pl.multiple_of(i * W_ROWS, W_ROWS), W_ROWS)]
-        kvd_copy(i).wait()
-        kd[:, :KV_DOWN] += lax.dot_general(lhs, kvd_buf[lax.rem(i, KV_SLOTS)], trans, preferred_element_type=jnp.float32)
-        down_copy(i).wait()
-        qd[...] += jnp.dot(lhs, w_buf[lax.rem(i, W_SLOTS), :, :Q_LAT], preferred_element_type=jnp.float32)
-
-        @pl.when(i + KV_SLOTS < N_DOWN)
-        def _():
-            kvd_copy(i + KV_SLOTS).start()
-
-        @pl.when(i + W_SLOTS < N_DOWN)
-        def _():
-            down_copy(i + W_SLOTS).start()
-
-    for s in range(N_DOWN, N_DOWN + W_SLOTS):
-        if s < FIRST_OUT:
-            up_copy(jnp.int32(s)).start()
-        if s == FIRST_OUT:
-            wkv_copy.start()
-        if s >= FIRST_OUT:
-            out_copy(jnp.int32(s)).start()
-
+    row16 = lax.broadcasted_iota(jnp.int32, (ROWS, 128), 0)
     lane16 = lax.broadcasted_iota(jnp.int32, (ROWS, 128), 1)
-    t0, t1 = tab_in[0], tab_in[1]
+    freq = jnp.zeros((ROWS, 128), jnp.float32)
+    for i in range(ROPE_DIM // 2):
+        freq = jnp.where(lax.rem(lane16, ROPE_DIM // 2) == i, ROPE_BASE ** (-i / (ROPE_DIM // 2)), freq)
+    tabs = []
+    for mb, p_ref in enumerate((pos_one, pos_two)):
+        at = jnp.zeros((ROWS, 128), jnp.float32)
+        for i in range(ROWS):
+            at = jnp.where(row16 == i, p_ref[i].astype(jnp.float32), at)
+        angle = at * freq
+        tabs.append(jnp.where(lane16 < 32, jnp.cos(angle), jnp.where(lane16 < 64, jnp.sin(angle), at)))
+        tab_ref[mb, z, c] = tabs[mb]
+    t0, t1 = tabs
     cos2 = jnp.where(lane16 < 32, t0, jnp.where(lane16 < 64, pltpu.roll(t0, 32, 1), jnp.where(lane16 < 96, pltpu.roll(t1, 64, 1), pltpu.roll(t1, 96, 1))))
     sin_hi = jnp.where((lane16 >= 32) & (lane16 < 64), t0, jnp.where(lane16 >= 96, pltpu.roll(t1, 64, 1), 0.0))
     sin_lo = jnp.where(lane16 < 32, -pltpu.roll(t0, 96, 1), jnp.where((lane16 >= 64) & (lane16 < 96), -pltpu.roll(t1, 32, 1), 0.0))
-    u = kd[:, :KV_LAT]
-    lat = (u * lax.rsqrt(jnp.mean(u * u, axis=-1, keepdims=True) + NORM_EPS) * gain_kv[...]).astype(jnp.bfloat16)
+
+    kd[...] = jnp.zeros_like(kd)
+    for i in range(2):
+        x_copy(i).wait()
+    for s in range(N_KV):
+        rhs = xs[:, s * HALF_N:(s + 1) * HALF_N]
+        lat_copy(s).wait()
+        kd[:KV_LAT, :2 * ROWS] += lax.dot_general(w_buf[s], rhs, trans, preferred_element_type=jnp.float32)
+        kr_copy(s).wait()
+        kd[KV_LAT:KV_DOWN, :2 * ROWS] += lax.dot_general(kr_buf[s], rhs, trans, preferred_element_type=jnp.float32)
+        down_copy(jnp.int32(s + W_SLOTS)).start()
+    raw = jnp.transpose(kd[...])[:2 * ROWS]
+    u = raw[:, :KV_LAT]
+    lat = (u * lax.rsqrt(jnp.mean(u * u, axis=-1, keepdims=True) + NORM_EPS) * gain_kv[...].astype(jnp.float32)[None]).astype(jnp.bfloat16)
     kv_ref[z, y, x, c, :, 0:KV_LAT] = lat[:ROWS]
     kv_ref[z, y, x, c, :, KV_LAT:2 * KV_LAT] = lat[ROWS:]
-    rot = jnp.where(lane16 < 64, kd[:ROWS, KV_LAT:], pltpu.roll(kd[ROWS:, KV_LAT:], 64, 1))
+    rot = jnp.where(lane16 < 64, raw[:ROWS, KV_LAT:], pltpu.roll(raw[ROWS:, KV_LAT:], 64, 1))
     rot = rot * cos2 + pltpu.roll(rot, 32, 1) * sin_hi + pltpu.roll(rot, 96, 1) * sin_lo
     kv_ref[z, y, x, c, :, 2 * KV_LAT:] = rot.astype(jnp.bfloat16)
-    v = qd[...]
-    q_lat = (v * lax.rsqrt(jnp.mean(v * v, axis=-1, keepdims=True) + NORM_EPS) * gain_q[...]).astype(jnp.bfloat16)
-    q_ref[:, z, c] = q_lat.reshape(2, ROWS, Q_LAT)
+    qd[...] = jnp.zeros_like(qd)
     pl.semaphore_wait(barrier, 10)
+
+    def q_down(lo, hi):
+        @pl.loop(lo, hi)
+        def _(i):
+            s = i + N_KV
+            lhs = xs[:, pl.ds(pl.multiple_of(i * W_ROWS, W_ROWS), W_ROWS)]
+            down_copy(s).wait()
+            qd[...] += jnp.dot(lhs, w_buf[lax.rem(s, W_SLOTS), :, :Q_LAT], preferred_element_type=jnp.float32)
+
+            @pl.when(s + W_SLOTS < FIRST_UP)
+            def _():
+                down_copy(s + W_SLOTS).start()
 
     def kv_piece(color, phase, at, core, half=None):
         (lo, hi), order = COLORS[color]
@@ -204,24 +216,44 @@
                 kv_copy(color, phase, k, shifted(pos, COLORS[color][1][phase], RING - k), other).wait_recv()
 
     start_phase(0)
-    for k in (1, 3, 2):
+    q_down(0, N_DOWN // 2)
+    wait_phase(0)
+    start_phase(1)
+    q_down(N_DOWN // 2, N_DOWN)
+    for s in range(FIRST_UP, FIRST_UP + W_SLOTS):
+        if s < FIRST_OUT:
+            up_copy(jnp.int32(s)).start()
+        if s == FIRST_OUT:
+            wkv_copy.start()
+        if s >= FIRST_OUT:
+            out_copy(jnp.int32(s)).start()
+    v = qd[...]
+    q_lat = (v * lax.rsqrt(jnp.mean(v * v, axis=-1, keepdims=True) + NORM_EPS) * gain_q[...].astype(jnp.float32)[None]).astype(jnp.bfloat16)
+    q_ref[:, z, c] = q_lat.reshape(2, ROWS, Q_LAT)
+    for k in (2, 1, 3):
         to = device(*shifted(pos, 0, k), c)
         t_copy(z, c, to, t_send.at[k - 1], t_recv.at[k - 1]).start()
         q_copy(z, c, to, q_send.at[k - 1], q_recv.at[k - 1]).start()
     t_copy(z, c, other, dq_send.at[0, 0], dq_recv.at[0, 0]).start()
     q_copy(z, c, other, dq_send.at[1, 0], dq_recv.at[1, 0]).start()
-    wait_phase(0)
-    start_phase(1)
+    wait_phase(1)
+    start_phase(2)
+    for color in range(3):
+        pass_copy(color, 0, pos, c).start()
     for k in (1, 3, 2):
         zz = lax.rem(z + RING - k, RING)
         t_copy(zz, c, other, t_send.at[k - 1], t_recv.at[k - 1]).wait_recv()
         t_copy(zz, c, other, dq_send.at[0, k], dq_recv.at[0, k]).start()
         q_copy(zz, c, other, q_send.at[k - 1], q_recv.at[k - 1]).wait_recv()
         q_copy(zz, c, other, dq_send.at[1, k], dq_recv.at[1, k]).start()
-    wait_phase(1)
-    start_phase(2)
-    for color in range(3):
-        pass_copy(color, 0, pos, c).start()
+
+    for k in (1, 3):
+        for color in (1, 2, 0):
+            axis = COLORS[color][1][2]
+            source = shifted(pos, axis, RING - k)
+            kv_copy(color, 2, k, source, other).wait_recv()
+            relay_copy(color, k // 2, source, device(*shifted(pos, axis, k), c)).start()
+            pass_copy(color, k, source, c).start()
     for k in range(RING):
         zz = lax.rem(z + RING - k, RING)
         t_copy(zz, 1 - c, other, dq_send.at[0, k], dq_recv.at[0, k]).wait()
@@ -247,7 +279,7 @@
         out = lax.dot_general(part.astype(jnp.bfloat16), w_k, (((1,), (1,)), ((), ())), preferred_element_type=jnp.float32)
         q_eff[:, :, head, :, :KV_LAT] = out.astype(jnp.bfloat16).reshape(2, RING, UNIT, KV_LAT)
 
-    for s in range(N_DOWN, FIRST_OUT):
+    for s in range(FIRST_UP, FIRST_OUT):
         up_copy(jnp.int32(s)).wait()
     wkv_copy.wait()
 
@@ -257,7 +289,7 @@
             cols = pl.ds(pl.multiple_of(p * (2 * QK_DIM), 128), 2 * QK_DIM)
             f = jnp.zeros((G_ROWS, 2 * QK_DIM), jnp.float32)
             for i in range(N_UP):
-                f = f + jnp.dot(q2[:, i * W_ROWS:(i + 1) * W_ROWS], w_buf[(N_DOWN + i) % W_SLOTS, :, cols],
+                f = f + jnp.dot(q2[:, i * W_ROWS:(i + 1) * W_ROWS], w_buf[(FIRST_UP + i) % W_SLOTS, :, cols],
                                 preferred_element_type=jnp.float32)
             head = p * 2
             put_nope(head, f[:, :128])
@@ -268,16 +300,9 @@
             put_rope(head + 1, last)
 
     queries(0, G_HEADS // 2)
-    for s in range(N_DOWN + W_SLOTS, FIRST_OUT + W_SLOTS):
+    for s in range(FIRST_UP + W_SLOTS, FIRST_OUT + W_SLOTS):
         out_copy(jnp.int32(s)).start()
 
-    for k in (1, 3):
-        for color in range(3):
-            axis = COLORS[color][1][2]
-            source = shifted(pos, axis, RING - k)
-            kv_copy(color, 2, k, source, other).wait_recv()
-            relay_copy(color, k // 2, source, device(*shifted(pos, axis, k), c)).start()
-            pass_copy(color, k, source, c).start()
     for color in range(3):
         source = shifted(pos, COLORS[color][1][2], 2)
         for half in range(2):
@@ -321,11 +346,13 @@
             o = jnp.dot(e, keys, preferred_element_type=jnp.float32).reshape(G_HEADS, UNIT, KV_LAT)
             q_eff[mb, zz, :, :, :KV_LAT] = (o / total).astype(jnp.bfloat16)
 
-        @pl.loop(0, G_HEADS)
-        def _(h):
-            w_v = wkv[:, pl.ds(pl.multiple_of(h * 256 + 128, 128), 128)]
-            o_h = jnp.dot(q_eff[mb, :, h, :, :KV_LAT].reshape(RING * UNIT, KV_LAT), w_v, preferred_element_type=jnp.float32)
-            o_ref[mb, :, :, :, pl.ds(pl.multiple_of(h * 128, 128), 128)] = o_h.astype(jnp.bfloat16).reshape(RING, 2, ROWS, V_DIM)
+        @pl.loop(0, G_HEADS // 4)
+        def _(g):
+            for i in range(4):
+                h = g * 4 + i
+                w_v = wkv[:, pl.ds(pl.multiple_of(h * 256 + 128, 128), 128)]
+                o_h = jnp.dot(q_eff[mb, :, h, :, :KV_LAT].reshape(RING * UNIT, KV_LAT), w_v, preferred_element_type=jnp.float32)
+                o_ref[mb, :, :, :, pl.ds(pl.multiple_of(h * 128, 128), 128)] = o_h.astype(jnp.bfloat16).reshape(RING, 2, ROWS, V_DIM)
 
         for k in (1, 3, 2):
             zz = lax.rem(z + k, RING)
@@ -368,7 +395,7 @@
     acc4 = acc.reshape(2, 2, ROWS, HALF_N)
     my_cols = pl.ds(pl.multiple_of(c * HALF_N, 128), HALF_N)
     their_cols = pl.ds(pl.multiple_of((1 - c) * HALF_N, 128), HALF_N)
-    outs = (y_one, y_two)
+    outs = (y_ref.at[0], y_ref.at[1])
 
     def y_copy(mb, cols):
         return pltpu.make_async_remote_copy(
@@ -402,22 +429,27 @@
         y_copy(mb, their_cols).wait()
 
 
-def block(x_one, x_two, gain_q, gain_kv, tab, w_qdown, w_kvdown, w_qup, w_kvup, w_out):
+def copy_kernel(y_ref, y_one, y_two):
+    y_one[...] = y_ref[0]
+    y_two[...] = y_ref[1]
+
+
+def block(pos_one, pos_two, gain_q, gain_kv, x_one, x_two, w_qdown, w_kvdown, w_qup, w_kvup, w_out):
     dma = pltpu.SemaphoreType.DMA
     vmem = pl.BlockSpec(memory_space=pltpu.VMEM)
+    smem = pl.BlockSpec(memory_space=pltpu.SMEM)
     hbm = pl.BlockSpec(memory_space=pl.ANY)
-    y_shape = jax.ShapeDtypeStruct((ROWS, D_MODEL), jnp.bfloat16)
     bf, f32 = jnp.bfloat16, jnp.float32
-    return pl.pallas_call(
+    y = pl.pallas_call(
         block_kernel,
-        out_shape=(y_shape, y_shape),
-        in_specs=[vmem] * 5 + [hbm] * 5,
-        out_specs=(vmem, vmem),
+        out_shape=jax.ShapeDtypeStruct((2, ROWS, D_MODEL), bf),
+        in_specs=[smem] * 2 + [vmem] * 2 + [hbm] * 7,
+        out_specs=vmem,
         scratch_shapes=[
             pltpu.VMEM((2 * ROWS, D_MODEL), bf),
             pltpu.VMEM((2 * ROWS, Q_LAT), f32),
-            pltpu.VMEM((2 * ROWS, KV_LAT + 128), f32),
-            pltpu.VMEM((KV_SLOTS, KV_DOWN, W_ROWS), bf),
+            pltpu.VMEM((KV_LAT + 128, 128), f32),
+            pltpu.VMEM((N_KV, ROPE_DIM, HALF_N), bf),
             pltpu.VMEM((W_SLOTS, W_ROWS, HALF_N), bf),
             pltpu.VMEM((KV_LAT, G_HEADS * 256), bf),
             pltpu.VMEM((RING, RING, RING, 2, ROWS, KV_W), bf),
@@ -428,22 +460,16 @@
             pltpu.VMEM((GROUP, 2, 2, ROWS, K_COLS), bf),
             pltpu.VMEM((OUT_ROWS, HALF_N), f32),
             pltpu.VMEM((2, ROWS, HALF_N), bf),
-            dma((W_SLOTS,)), dma((KV_SLOTS,)), dma,
+            dma((2,)), dma((W_SLOTS,)), dma((N_KV,)), dma,
             dma((3, 3, 3)), dma((3, 3, 3)), dma((3, 2)), dma((3, 2)), dma((3, 4)), dma((3, 4)),
             dma((3,)), dma((3,)), dma((3,)), dma((3,)), dma((2, 4)), dma((2, 4)),
             dma((2, 3)), dma((2, 3)), dma((2, 4)), dma((2, 4)), dma((2,)), dma((2,)),
         ],
         compiler_params=pltpu.CompilerParams(collective_id=0, has_side_effects=True, vmem_limit_bytes=67043328),
         name="latent_attention_block",
-    )(x_one, x_two, gain_q, gain_kv, tab, w_qdown, w_kvdown, w_qup, w_kvup, w_out)
-
-
-def tables(pos_one, pos_two):
-    lane = np.arange(128)
-    inv_freq = (ROPE_BASE ** (-(lane % 32) / (ROPE_DIM // 2))).astype(np.float32)
-    pos = jnp.stack([pos_one, pos_two]).astype(jnp.float32)[:, :, None]
-    angles = pos * inv_freq
-    return jnp.where(lane < 32, jnp.cos(angles), jnp.where(lane < 64, jnp.sin(angles), pos))
+    )(pos_one, pos_two, gain_q, gain_kv, x_one, x_two, w_qdown, w_kvdown, w_qup, w_kvup, w_out)
+    y_shape = jax.ShapeDtypeStruct((ROWS, D_MODEL), bf)
+    return pl.pallas_call(copy_kernel, out_shape=(y_shape, y_shape), in_specs=[vmem], out_specs=(vmem, vmem), name="results")(y)
 
 
 def solution(mesh):
@@ -451,7 +477,6 @@
     idx_spec = P(('dp', 'sp'))
 
     def local_body(x_one, seg_one, pos_one, x_two, seg_two, pos_two, w_qdown, gain_q, w_qup, w_kvdown, gain_kv, w_kvup, w_out):
-        gains = (gain_q.astype(jnp.float32)[None], gain_kv.astype(jnp.float32)[None])
-        return block(x_one, x_two, *gains, tables(pos_one, pos_two), w_qdown, w_kvdown.T, w_qup, w_kvup, w_out)
+        return block(pos_one, pos_two, gain_q, gain_kv, x_one, x_two, w_qdown, w_kvdown.T, w_qup, w_kvup, w_out)
 
     return jax.shard_map(local_body, mesh=mesh, in_specs=(tok_spec, idx_spec, idx_spec, tok_spec, idx_spec, idx_spec, P(), P(), P(), P(), P(), P(), P()), out_specs=(tok_spec, tok_spec), check_vma=False)

time: 106 us -> 93.3 us (0.88)
  local copies, waits for them, and re-layouts: 4.56 us -> 0 us
  Pallas kernels: 96.8 us -> 92.5 us
  other arithmetic: 3.39 us -> 0 us
    pallas_call x1 -> x2, Pallas kernels: 96.8 us -> 92.5 us  [the longest x1 90.7 us: block(): pl.pallas_call(block_kernel, out_shape=jax.ShapeDtypeStruct((2, ROWS, D_M...]
    unnamed x2 -> x0, local copies, waits for them, and re-layouts: 3.28 us -> none
    select_n x1 -> x0, other arithmetic: 1.44 us -> none  [tables(): jnp.where(lane < 32, jnp.cos(angles), jnp.where(lane < 64, jnp.sin(angles...]
    broadcast_in_dim x1 -> x0, local copies, waits for them, and re-layouts: 1.28 us -> none  [local_body(): gain_q.astype(jnp.float32)[None]]
    broadcast_in_dim x1 -> x0, other arithmetic: 1.27 us -> none  [local_body(): gain_kv.astype(jnp.float32)[None]]
where the time goes in v3:
time: 93.3 us; the launch traced here: 93.1 us
  Pallas kernels  92.5 us (99%)
    pallas_call x1, Pallas kernels, block(): pl.pallas_call(block_kernel, out_shape=jax.ShapeDtypeStruct((2, ROWS, D_M...  90.7 us

profile of v3, /device:TPU:1, one launch (start us, length us, event | category | flops | bytes accessed | tf_op | source)
XLA Modules:
  0.0 93.1 jit_solution(15005586834636703442)
XLA Ops:
  0.6 90.7 %latent_attention_block.1.y_ref = bf16[2,16,7168]{2,1,0:T(8,128)(2,1)} custom-call(s32[16]{0:T(128)} %pos_one.1, s32[16]{0:T(128)} %pos_two.1, bf16[1536]{0:T(1024)(128)(2,1)} %gain_q.1, bf16[512]{0:T(512)(128)(2,1)} %gain_kv.1, bf16[16,7168]{1,0:T(8,128)(2,1)} %x_one.1, bf16[16,7168]{1,0:T(8,128)(2,1)} %x_two.1, bf16[7168,1536]{1,0:T(8,128)(2,1)} %wqd.1, ...), custom_call_target="tpu_custom_call" | custom-call | tf_op jit(solution)/shard_map/latent_attention_block/pallas_call | solution.py:443
  91.3 1.8 %results.1 = (bf16[16,7168]{1,0:T(8,128)(2,1)}, bf16[16,7168]{1,0:T(8,128)(2,1)}) custom-call(bf16[2,16,7168]{2,1,0:T(8,128)(2,1)} %latent_attention_block.1.y_ref), custom_call_target="tpu_custom_call" | custom-call | tf_op jit(solution)/shard_map/results/pallas_call | solution.py:472

commit v4 on v3

--- a/solution.py
+++ b/solution.py
@@ -34,7 +34,7 @@
 COLORS = (((0, 256), (2, 1, 0)), ((256, 640), (1, 0, 2)), ((640, 1152), (0, 2, 1)))
 
 W_ROWS = 512
-W_SLOTS = 8
+W_SLOTS = 9
 N_KV = 2
 N_DOWN = D_MODEL // W_ROWS
 N_UP = Q_LAT // W_ROWS
@@ -116,8 +116,7 @@
     for s in range(N_KV):
         lat_copy(s).start()
         kr_copy(s).start()
-    for s in range(N_KV, W_SLOTS):
-        down_copy(jnp.int32(s)).start()
+    down_copy(jnp.int32(N_KV)).start()
 
     barrier = pltpu.get_barrier_semaphore()
     for axis in range(3):
@@ -149,6 +148,9 @@
     for s in range(N_KV):
         rhs = xs[:, s * HALF_N:(s + 1) * HALF_N]
         lat_copy(s).wait()
+        if s == 0:
+            for i in range(N_KV + 1, W_SLOTS):
+                down_copy(jnp.int32(i)).start()
         kd[:KV_LAT, :2 * ROWS] += lax.dot_general(w_buf[s], rhs, trans, preferred_element_type=jnp.float32)
         kr_copy(s).wait()
         kd[KV_LAT:KV_DOWN, :2 * ROWS] += lax.dot_general(kr_buf[s], rhs, trans, preferred_element_type=jnp.float32)
@@ -285,21 +287,25 @@
 
     def queries(lo, hi):
         @pl.loop(lo, hi)
-        def _(p):
-            cols = pl.ds(pl.multiple_of(p * (2 * QK_DIM), 128), 2 * QK_DIM)
-            f = jnp.zeros((G_ROWS, 2 * QK_DIM), jnp.float32)
-            for i in range(N_UP):
-                f = f + jnp.dot(q2[:, i * W_ROWS:(i + 1) * W_ROWS], w_buf[(FIRST_UP + i) % W_SLOTS, :, cols],
-                                preferred_element_type=jnp.float32)
-            head = p * 2
-            put_nope(head, f[:, :128])
-            put_rope(head, f[:, 128:256])
-            mid = pltpu.roll(f[:, 128:256], 64, 1)
-            last = pltpu.roll(f[:, 256:384], 64, 1)
-            put_nope(head + 1, jnp.where(lane < 64, mid, last))
-            put_rope(head + 1, last)
-
-    queries(0, G_HEADS // 2)
+        def _(g):
+            parts = []
+            for i in range(2):
+                cols = pl.ds(pl.multiple_of((2 * g + i) * (2 * QK_DIM), 128), 2 * QK_DIM)
+                f = jnp.zeros((G_ROWS, 2 * QK_DIM), jnp.float32)
+                for n in range(N_UP):
+                    f = f + jnp.dot(q2[:, n * W_ROWS:(n + 1) * W_ROWS], w_buf[(FIRST_UP + n) % W_SLOTS, :, cols],
+                                    preferred_element_type=jnp.float32)
+                parts.append(f)
+            for i, f in enumerate(parts):
+                head = 4 * g + 2 * i
+                put_nope(head, f[:, :128])
+                put_rope(head, f[:, 128:256])
+                mid = pltpu.roll(f[:, 128:256], 64, 1)
+                last = pltpu.roll(f[:, 256:384], 64, 1)
+                put_nope(head + 1, jnp.where(lane < 64, mid, last))
+                put_rope(head + 1, last)
+
+    queries(0, G_HEADS // 4)
     for s in range(FIRST_UP + W_SLOTS, FIRST_OUT + W_SLOTS):
         out_copy(jnp.int32(s)).start()
 

time: 93.3 us -> 88.5 us (0.949)
  Pallas kernels: 92.5 us -> 87.6 us
    pallas_call x1, Pallas kernels: 90.7 us -> 85.8 us  [block(): pl.pallas_call(block_kernel, out_shape=jax.ShapeDtypeStruct((2, ROWS, D_M...]
where the time goes in v4:
time: 88.5 us; the launch traced here: 88.3 us
  Pallas kernels  87.6 us (99%)
    pallas_call x1, Pallas kernels, block(): pl.pallas_call(block_kernel, out_shape=jax.ShapeDtypeStruct((2, ROWS, D_M...  85.8 us
    pallas_call x1, Pallas kernels, block(): pl.pallas_call(copy_kernel, out_shape=(y_shape, y_shape), in_specs=[vmem]...  1.8 us

profile of v4, /device:TPU:1, one launch (start us, length us, event | category | flops | bytes accessed | tf_op | source)
XLA Modules:
  0.0 88.3 jit_solution(3773777837198976967)
XLA Ops:
  0.6 85.8 %latent_attention_block.1.y_ref = bf16[2,16,7168]{2,1,0:T(8,128)(2,1)} custom-call(s32[16]{0:T(128)} %pos_one.1, s32[16]{0:T(128)} %pos_two.1, bf16[1536]{0:T(1024)(128)(2,1)} %gain_q.1, bf16[512]{0:T(512)(128)(2,1)} %gain_kv.1, bf16[16,7168]{1,0:T(8,128)(2,1)} %x_one.1, bf16[16,7168]{1,0:T(8,128)(2,1)} %x_two.1, bf16[7168,1536]{1,0:T(8,128)(2,1)} %wqd.1, ...), custom_call_target="tpu_custom_call" | custom-call | tf_op jit(solution)/shard_map/latent_attention_block/pallas_call | solution.py:449
  86.5 1.8 %results.1 = (bf16[16,7168]{1,0:T(8,128)(2,1)}, bf16[16,7168]{1,0:T(8,128)(2,1)}) custom-call(bf16[2,16,7168]{2,1,0:T(8,128)(2,1)} %latent_attention_block.1.y_ref), custom_call_target="tpu_custom_call" | custom-call | tf_op jit(solution)/shard_map/results/pallas_call | solution.py:478

commit v5 on v4

--- a/solution.py
+++ b/solution.py
@@ -27,24 +27,25 @@
 UNIT = 2 * ROWS
 G_ROWS = 2 * RING * UNIT
 HALF_N = D_MODEL // 2
-OUT_ROWS = 2 * UNIT
+OUT_N = D_MODEL // 4
+OUT_ROWS = 4 * UNIT
 K_COLS = G_HEADS * V_DIM
 MESH = pl.DeviceIdType.MESH
 
 COLORS = (((0, 256), (2, 1, 0)), ((256, 640), (1, 0, 2)), ((640, 1152), (0, 2, 1)))
 
 W_ROWS = 512
-W_SLOTS = 9
+W_SLOTS = 8
 N_KV = 2
 N_DOWN = D_MODEL // W_ROWS
 N_UP = Q_LAT // W_ROWS
-N_OUT = HEADS * V_DIM // W_ROWS
+N_OUT = HEADS * V_DIM // (2 * W_ROWS)
 FIRST_UP = N_KV + N_DOWN
 FIRST_OUT = FIRST_UP + N_UP
 N_CHUNKS = FIRST_OUT + N_OUT
-PER_RANK = K_COLS // W_ROWS
-
-ORDER = ((0, 0), (0, 1), (1, 0), (3, 0), (1, 1), (2, 0), (3, 1), (2, 1))
+PER_RANK = K_COLS // (2 * W_ROWS)
+
+ORDER = ((0, 0), (0, 1), (1, 0), (3, 0), (1, 1), (3, 1), (2, 0), (2, 1))
 
 
 def coords():
@@ -64,12 +65,14 @@
 
 def block_kernel(pos_one, pos_two, gain_q, gain_kv, x_one, x_two, wqd, wkvd, wqu, wkvu, wout, y_ref,
                  xs, qd, kd, kr_buf, w_buf, wkv, kv_ref, q_ref, tab_ref, q_eff, o_ref, o_all, acc, y_send,
-                 x_sem, w_sem, kr_sem, wkv_sem, kv_send, kv_recv, r_send, r_recv, d_send, d_recv,
+                 x_sem, w_sem, w_sem2, kr_sem, wkv_sem, kv_send, kv_recv, r_send, r_recv, d_send, d_recv,
                  q_send, q_recv, t_send, t_recv, dq_send, dq_recv, a_send, a_recv, p_send, p_recv, y_ssem, y_rsem):
     z, y, x, c = coords()
     pos = (z, y, x)
     rank = z * 2 + c
     other = device(z, y, x, 1 - c)
+    pair, member = z // 2, lax.rem(z, 2)
+    mate = 2 * pair + 1 - member
     trans = (((1,), (1,)), ((), ()))
 
     def rank_at(j):
@@ -101,12 +104,18 @@
             wqu.at[pl.ds(pl.multiple_of((s - FIRST_UP) * W_ROWS, W_ROWS), W_ROWS), pl.ds(pl.multiple_of(rank * width, 128), width)],
             w_buf.at[slot, :, pl.ds(0, width)], w_sem.at[slot])
 
-    def out_copy(s):
+    def out_copies(s):
         slot = lax.rem(s, W_SLOTS)
         t = s - FIRST_OUT
-        row = pl.multiple_of(rank_at(t // PER_RANK) * K_COLS + lax.rem(t, PER_RANK) * W_ROWS, W_ROWS)
-        return pltpu.make_async_copy(
-            wout.at[pl.ds(row, W_ROWS), pl.ds(pl.multiple_of(c * HALF_N, 128), HALF_N)], w_buf.at[slot], w_sem.at[slot])
+        row = rank_at(t // PER_RANK) * K_COLS + lax.rem(t, PER_RANK) * (2 * W_ROWS)
+        cols = pl.ds(pl.multiple_of((member * 2 + c) * OUT_N, 128), OUT_N)
+        return [pltpu.make_async_copy(
+            wout.at[pl.ds(pl.multiple_of(row + h * W_ROWS, W_ROWS), W_ROWS), cols],
+            w_buf.at[slot, :, pl.ds(h * OUT_N, OUT_N)], sem.at[slot]) for h, sem in enumerate((w_sem, w_sem2))]
+
+    def out_start(s):
+        for copy in out_copies(s):
+            copy.start()
 
     wkv_copy = pltpu.make_async_copy(
         wkvu.at[:, pl.ds(pl.multiple_of(rank * (G_HEADS * 256), 128), G_HEADS * 256)], wkv, wkv_sem)
@@ -123,6 +132,7 @@
         for k in range(1, RING):
             pl.semaphore_signal(barrier, inc=1, device_id=device(*shifted(pos, axis, k), c), device_id_type=MESH)
     pl.semaphore_signal(barrier, inc=1, device_id=other, device_id_type=MESH)
+    pl.semaphore_signal(barrier, inc=1, device_id=device(mate, y, x, 1 - c), device_id_type=MESH)
 
     row16 = lax.broadcasted_iota(jnp.int32, (ROWS, 128), 0)
     lane16 = lax.broadcasted_iota(jnp.int32, (ROWS, 128), 1)
@@ -164,7 +174,7 @@
     rot = rot * cos2 + pltpu.roll(rot, 32, 1) * sin_hi + pltpu.roll(rot, 96, 1) * sin_lo
     kv_ref[z, y, x, c, :, 2 * KV_LAT:] = rot.astype(jnp.bfloat16)
     qd[...] = jnp.zeros_like(qd)
-    pl.semaphore_wait(barrier, 10)
+    pl.semaphore_wait(barrier, 11)
 
     def q_down(lo, hi):
         @pl.loop(lo, hi)
@@ -228,7 +238,7 @@
         if s == FIRST_OUT:
             wkv_copy.start()
         if s >= FIRST_OUT:
-            out_copy(jnp.int32(s)).start()
+            out_start(jnp.int32(s))
     v = qd[...]
     q_lat = (v * lax.rsqrt(jnp.mean(v * v, axis=-1, keepdims=True) + NORM_EPS) * gain_q[...].astype(jnp.float32)[None]).astype(jnp.bfloat16)
     q_ref[:, z, c] = q_lat.reshape(2, ROWS, Q_LAT)
@@ -307,7 +317,7 @@
 
     queries(0, G_HEADS // 4)
     for s in range(FIRST_UP + W_SLOTS, FIRST_OUT + W_SLOTS):
-        out_copy(jnp.int32(s)).start()
+        out_start(jnp.int32(s))
 
     for color in range(3):
         source = shifted(pos, COLORS[color][1][2], 2)
@@ -320,7 +330,7 @@
 
     def ring_copy(mb, k, zz, src_rank, to):
         return pltpu.make_async_remote_copy(
-            src_ref=o_ref.at[mb, zz], dst_ref=o_all.at[src_rank, mb], send_sem=a_send.at[mb, k - 1],
+            src_ref=o_ref.at[mb, pl.ds(2 * (zz // 2), 2)], dst_ref=o_all.at[src_rank, mb], send_sem=a_send.at[mb, k - 1],
             recv_sem=a_recv.at[mb, k - 1], device_id=to, device_id_type=MESH)
 
     def pair_copy(mb, k, src_rank, src):
@@ -363,10 +373,18 @@
         for k in (1, 3, 2):
             zz = lax.rem(z + k, RING)
             ring_copy(mb, k, zz, rank, device(zz, y, x, c)).start()
-        pair_copy(mb, 0, rank, o_ref.at[mb, z]).start()
-
-    o_all[rank] = o_ref[:, z]
+        pair_copy(mb, 0, rank, o_ref.at[mb, pl.ds(2 * pair, 2)]).start()
+
+    o_all[rank] = o_ref[:, pl.ds(2 * pair, 2)]
     acc[...] = jnp.zeros_like(acc)
+
+    def arrive(mb, k):
+        src_rank = lax.rem(z + RING - k, RING) * 2 + c
+        ring_copy(mb, k, z, src_rank, other).wait_recv()
+        pair_copy(mb, k, src_rank, o_all.at[src_rank, mb]).start()
+
+    arrive(0, 1)
+    arrive(0, 3)
 
     @pl.loop(0, N_OUT)
     def _(t):
@@ -375,45 +393,51 @@
                 continue
 
             @pl.when(t == i * PER_RANK)
-            def _(i=i, k=k, flip=flip):
-                src_rank = lax.rem(z + RING - k, RING) * 2 + (c if flip == 0 else 1 - c)
-                for mb in range(2):
-                    if flip == 0:
-                        ring_copy(mb, k, z, src_rank, other).wait_recv()
-                        pair_copy(mb, k, src_rank, o_all.at[src_rank, mb]).start()
-                    else:
+            def _(k=k, flip=flip):
+                if flip == 0:
+                    if k == 2:
+                        arrive(0, k)
+                    arrive(1, k)
+                else:
+                    src_rank = lax.rem(z + RING - k, RING) * 2 + 1 - c
+                    for mb in range(2):
                         pair_copy(mb, k, src_rank, o_all.at[src_rank, mb]).wait_recv()
 
         s = t + FIRST_OUT
-        cols = pl.ds(pl.multiple_of(lax.rem(t, PER_RANK) * W_ROWS, W_ROWS), W_ROWS)
-        lhs = o_all[rank_at(t // PER_RANK), :, :, :, cols].reshape(OUT_ROWS, W_ROWS)
-        out_copy(s).wait()
+        src = rank_at(t // PER_RANK)
+        k0 = lax.rem(t, PER_RANK) * (2 * W_ROWS)
+        lhs = [o_all[src, :, :, :, :, pl.ds(pl.multiple_of(k0 + h * W_ROWS, W_ROWS), W_ROWS)].reshape(OUT_ROWS, W_ROWS) for h in range(2)]
+        for copy in out_copies(s):
+            copy.wait()
         slot = lax.rem(s, W_SLOTS)
-        step_n = 512
-        for n in range(HALF_N // step_n):
-            part = slice(n * step_n, (n + 1) * step_n)
-            acc[:, part] += jnp.dot(lhs, w_buf[slot, :, part], preferred_element_type=jnp.float32)
+        for lo in range(0, OUT_N, 512):
+            hi = min(lo + 512, OUT_N)
+            acc[:, lo:hi] += (jnp.dot(lhs[0], w_buf[slot, :, lo:hi], preferred_element_type=jnp.float32)
+                              + jnp.dot(lhs[1], w_buf[slot, :, OUT_N + lo:OUT_N + hi], preferred_element_type=jnp.float32))
 
         @pl.when(s + W_SLOTS < N_CHUNKS)
         def _():
-            out_copy(s + W_SLOTS).start()
-
-    acc4 = acc.reshape(2, 2, ROWS, HALF_N)
-    my_cols = pl.ds(pl.multiple_of(c * HALF_N, 128), HALF_N)
-    their_cols = pl.ds(pl.multiple_of((1 - c) * HALF_N, 128), HALF_N)
-    outs = (y_ref.at[0], y_ref.at[1])
-
-    def y_copy(mb, cols):
+            out_start(s + W_SLOTS)
+
+    acc5 = acc.reshape(2, 2, 2, ROWS, OUT_N)
+    owners = ((member, 1 - c), (1 - member, c), (1 - member, 1 - c))
+
+    def col_part(mm, cc):
+        return pl.ds(pl.multiple_of((mm * 2 + cc) * OUT_N, 128), OUT_N)
+
+    def y_copy(d, cols):
+        mm, cc = owners[d]
         return pltpu.make_async_remote_copy(
-            src_ref=y_send.at[mb], dst_ref=outs[mb].at[:, cols], send_sem=y_ssem.at[mb], recv_sem=y_rsem.at[mb],
-            device_id=other, device_id_type=MESH)
-
+            src_ref=y_send.at[d], dst_ref=y_ref.at[:, :, cols], send_sem=y_ssem.at[d], recv_sem=y_rsem.at[d],
+            device_id=device(2 * pair + mm, y, x, cc), device_id_type=MESH)
+
+    for d in (2, 1, 0):
+        for mb in range(2):
+            y_send[d, mb] = acc5[mb, owners[d][0], owners[d][1]].astype(jnp.bfloat16)
     for mb in range(2):
-        y_send[mb] = acc4[mb, 1 - c].astype(jnp.bfloat16)
-    for mb in range(2):
-        outs[mb][:, my_cols] = acc4[mb, c].astype(jnp.bfloat16)
-    for mb in range(2):
-        y_copy(mb, my_cols).start()
+        y_ref[mb, :, col_part(member, c)] = acc5[mb, member, c].astype(jnp.bfloat16)
+    for d in (2, 1, 0):
+        y_copy(d, col_part(member, c)).start()
 
     for k in range(1, RING):
         t_copy(z, c, other, t_send.at[k - 1], t_recv.at[k - 1]).wait_send()
@@ -432,7 +456,8 @@
             ring_copy(mb, k, z, rank, other).wait_send()
         for k in range(RING):
             pair_copy(mb, k, rank, o_all.at[rank, mb]).wait_send()
-        y_copy(mb, their_cols).wait()
+    for d in range(3):
+        y_copy(d, col_part(*owners[d])).wait()
 
 
 def copy_kernel(y_ref, y_one, y_two):
@@ -463,13 +488,13 @@
             pltpu.VMEM((2, RING, 2, ROWS, 128), f32),
             pltpu.VMEM((2, RING, G_HEADS, UNIT, Q_W), bf),
             pltpu.VMEM((2, RING, 2, ROWS, K_COLS), bf),
-            pltpu.VMEM((GROUP, 2, 2, ROWS, K_COLS), bf),
-            pltpu.VMEM((OUT_ROWS, HALF_N), f32),
-            pltpu.VMEM((2, ROWS, HALF_N), bf),
-            dma((2,)), dma((W_SLOTS,)), dma((N_KV,)), dma,
+            pltpu.VMEM((GROUP, 2, 2, 2, ROWS, K_COLS), bf),
+            pltpu.VMEM((OUT_ROWS, OUT_N), f32),
+            pltpu.VMEM((3, 2, ROWS, OUT_N), bf),
+            dma((2,)), dma((W_SLOTS,)), dma((W_SLOTS,)), dma((N_KV,)), dma,
             dma((3, 3, 3)), dma((3, 3, 3)), dma((3, 2)), dma((3, 2)), dma((3, 4)), dma((3, 4)),
             dma((3,)), dma((3,)), dma((3,)), dma((3,)), dma((2, 4)), dma((2, 4)),
-            dma((2, 3)), dma((2, 3)), dma((2, 4)), dma((2, 4)), dma((2,)), dma((2,)),
+            dma((2, 3)), dma((2, 3)), dma((2, 4)), dma((2, 4)), dma((3,)), dma((3,)),
         ],
         compiler_params=pltpu.CompilerParams(collective_id=0, has_side_effects=True, vmem_limit_bytes=67043328),
         name="latent_attention_block",

time: 88.5 us -> 85.7 us (0.968)
  the two profiles are of different devices: /device:TPU:1 before, /device:TPU:66 now
where the time goes in v5:
time: 85.7 us; the launch traced here: 85.5 us
  Pallas kernels  84.8 us (99%)
    pallas_call x1, Pallas kernels, block(): pl.pallas_call(block_kernel, out_shape=jax.ShapeDtypeStruct((2, ROWS, D_M...  83 us
    pallas_call x1, Pallas kernels, block(): pl.pallas_call(copy_kernel, out_shape=(y_shape, y_shape), in_specs=[vmem]...  1.8 us

profile of v5, /device:TPU:66, one launch (start us, length us, event | category | flops | bytes accessed | tf_op | source)
XLA Modules:
  0.0 85.5 jit_solution(8665409375657933401)
XLA Ops:
  0.6 83.0 %latent_attention_block.1.y_ref = bf16[2,16,7168]{2,1,0:T(8,128)(2,1)} custom-call(s32[16]{0:T(128)} %pos_one.1, s32[16]{0:T(128)} %pos_two.1, bf16[1536]{0:T(1024)(128)(2,1)} %gain_q.1, bf16[512]{0:T(512)(128)(2,1)} %gain_kv.1, bf16[16,7168]{1,0:T(8,128)(2,1)} %x_one.1, bf16[16,7168]{1,0:T(8,128)(2,1)} %x_two.1, bf16[7168,1536]{1,0:T(8,128)(2,1)} %wqd.1, ...), custom_call_target="tpu_custom_call" | custom-call | tf_op jit(solution)/shard_map/latent_attention_block/pallas_call | solution.py:474
  83.7 1.8 %results.1 = (bf16[16,7168]{1,0:T(8,128)(2,1)}, bf16[16,7168]{1,0:T(8,128)(2,1)}) custom-call(bf16[2,16,7168]{2,1,0:T(8,128)(2,1)} %latent_attention_block.1.y_ref), custom_call_target="tpu_custom_call" | custom-call | tf_op jit(solution)/shard_map/results/pallas_call | solution.py:503
